TPU v7x, 32 devices: a whole 2x2x4 slice. The times are simulated.
32 devices in a mesh: pool: 2 (over x), seq: 4 (over y, core), head: 4 (over z).
Axes of the slice: x: 2, y: 2, z: 4, core: 2. Of those that a mesh axis runs over, the one named last changes fastest.
Arguments:
- prompt: bfloat16 [8, 2048, 8192], P('pool', 'seq'), may hold values from -6 to 6
- key_value_weight: bfloat16 [8192, 2, 1024], P('seq', None, 'head'), may hold values from -0.0625 to 0.0625
- adapter_down_weight: bfloat16 [8192, 256], P('seq'), may hold values from -0.0625 to 0.0625
- adapter_up_weight: bfloat16 [8, 2, 16, 1024], P(None, None, None, 'head'), may hold values from -0.75 to 0.75
- request_adapter_index: int32 [8], P('pool'), may hold values from 0 to 7
- destination: int32 [8], replicated, may hold values from 0 to 3, as said below
- rotated_query: bfloat16 [384, 8192], P(('pool', 'seq'), 'head'), may hold values from -150 to 150
- key_value_cache: bfloat16 [384, 128, 2, 1024], P(('pool', 'seq'), None, None, 'head'), may hold values from -6 to 6
- current_key_value: bfloat16 [384, 2, 1024], P(('pool', 'seq'), None, 'head'), may hold values from -6 to 6
- cached_length: int32 [384], P(('pool', 'seq')), may hold values from 1 to 128
- row_adapter_index: int32 [384], P('pool'), may hold values from 0 to 7
- output_weight: bfloat16 [8192, 8192], P('head', 'seq'), may hold values from -0.0625 to 0.0625
- output_down_weight: bfloat16 [8192, 8, 16], P('head'), may hold values from -0.0625 to 0.0625
- output_up_weight: bfloat16 [8, 16, 8192], P(None, None, 'seq'), may hold values from -3.59375 to 3.59375
Outputs:
- handed: bfloat16 [8, 2, 2048, 2, 1024], P(('pool', 'seq'), None, None, None, 'head')
- decoded: bfloat16 [384, 8192], P(('pool', 'head'), 'seq')
Inputs may be any that keep to these rules, and one draw needn't show every extreme that they name: `destination`: among one pool's 4 requests no decode owner is named more than 2 times, and some owner exactly 2 times; in each pool owners 0 and 3 both receive requests.
All inputs are finite; a program needn't handle non-finite values.
Results may differ from a plain program's by a relative error of at most 0.0085.
Values may be sent and summed in bfloat16 or wider, within the bound.
A program may use at most 128 MiB of HBM per device.

v0:
```python
import jax
import jax.numpy as jnp
from jax import lax
from jax.experimental import pallas as pl
from jax.experimental.pallas import tpu as pltpu
from jax.sharding import PartitionSpec as P

HEAD_DIM = 128
ADAPTER_RANK = 16
ADAPTER_COUNT = 8
CAP = 2


def exchanged(value, axis, mask):
    pairs = [(source, source ^ mask) for source in range(lax.axis_size(axis))]
    return lax.ppermute(value, axis, pairs)


def gathered(value, axis, after=None):
    size = lax.axis_size(axis)
    index = lax.axis_index(axis)
    held = value[None]
    mask = size // 2
    arrived = None
    while mask >= 1:
        other = exchanged(held, axis, mask)
        if after is not None:
            other = lax.optimization_barrier((other, after))[0]
        arrived = other if arrived is None else arrived
        low_bit = (index // mask) % 2 == 0
        first = jnp.where(low_bit, held, other)
        second = jnp.where(low_bit, other, held)
        held = jnp.stack([first, second], axis=1).reshape((-1,) + value.shape)
        mask //= 2
    return held, arrived


def scattered_sum(value, axis):
    size = lax.axis_size(axis)
    index = lax.axis_index(axis)
    held = value.reshape((size, value.shape[0] // size) + value.shape[1:])
    mask = 1
    while mask < size:
        split = held.reshape((held.shape[0] // 2, 2) + held.shape[1:])
        low_bit = (index // mask) % 2 == 0
        keep = jnp.where(low_bit, split[:, 0], split[:, 1])
        give = jnp.where(low_bit, split[:, 1], split[:, 0])
        held = keep + exchanged(give, axis, mask)
        mask *= 2
    return held[0]


def attend_kernel(lengths, query_ref, cache_ref, key_ref, value_ref, out_ref):
    rows, positions = cache_ref.shape[0], cache_ref.shape[1]
    kv_heads = key_ref.shape[1]
    groups = query_ref.shape[1] // kv_heads
    start = pl.program_id(0) * rows
    lane = lax.broadcasted_iota(jnp.int32, (groups, 2 * positions), 1)
    factor = HEAD_DIM ** (-0.5)
    blocks, scores, owns = [], [], []
    for row in range(rows):
        pairs = cache_ref[row].reshape(2 * positions, kv_heads * HEAD_DIM)
        valid = (lane % 2 == 0) & (lane < 2 * lengths[start + row])
        for head in range(kv_heads):
            block = pairs[:, head * HEAD_DIM : (head + 1) * HEAD_DIM]
            query = query_ref[row, head * groups : (head + 1) * groups, :]
            own_key = key_ref[row, head : head + 1, :].astype(jnp.float32)
            own = jnp.sum(query.astype(jnp.float32) * own_key, axis=1, keepdims=True) * factor
            score = lax.dot_general(
                query, block, (((1,), (1,)), ((), ())), preferred_element_type=jnp.float32
            )
            blocks.append(block)
            scores.append(jnp.where(valid, score * factor, -1e30))
            owns.append(own)
    scores = jnp.concatenate(scores, axis=0)
    own = jnp.concatenate(owns, axis=0)
    highest = jnp.maximum(jnp.max(scores, axis=1, keepdims=True), own)
    raw = jnp.where(scores > -1e29, jnp.exp(scores - highest), 0.0)
    own_raw = jnp.exp(own - highest)
    total = jnp.sum(raw, axis=1, keepdims=True) + own_raw
    weights = pltpu.roll(raw / total, 1, 1).astype(jnp.bfloat16)
    own_weight = (own_raw / total).astype(jnp.bfloat16).astype(jnp.float32)
    for row in range(rows):
        for head in range(kv_heads):
            at = (row * kv_heads + head) * groups
            own_value = value_ref[row, head : head + 1, :].astype(jnp.float32)
            mixed = jnp.dot(
                weights[at : at + groups],
                blocks[row * kv_heads + head],
                preferred_element_type=jnp.float32,
            )
            out_ref[row, head * groups : (head + 1) * groups, :] = (
                mixed + own_weight[at : at + groups] * own_value
            ).astype(jnp.bfloat16)


def attend(query, cache, current, lengths):
    rows, positions, _, width = cache.shape
    kv_heads = width // HEAD_DIM
    heads = query.shape[1] // HEAD_DIM
    step = next(size for size in (8, 4, 2, 1) if rows % size == 0)
    query = query.reshape(rows, heads, HEAD_DIM)
    own_key = current[:, 0].reshape(rows, kv_heads, HEAD_DIM)
    own_value = current[:, 1].reshape(rows, kv_heads, HEAD_DIM)
    out = pl.pallas_call(
        attend_kernel,
        grid_spec=pltpu.PrefetchScalarGridSpec(
            num_scalar_prefetch=1,
            grid=(rows // step,),
            in_specs=[
                pl.BlockSpec((step, heads, HEAD_DIM), lambda i, _: (i, 0, 0)),
                pl.BlockSpec((step, positions, 2, width), lambda i, _: (i, 0, 0, 0)),
                pl.BlockSpec((step, kv_heads, HEAD_DIM), lambda i, _: (i, 0, 0)),
                pl.BlockSpec((step, kv_heads, HEAD_DIM), lambda i, _: (i, 0, 0)),
            ],
            out_specs=pl.BlockSpec((step, heads, HEAD_DIM), lambda i, _: (i, 0, 0)),
        ),
        out_shape=jax.ShapeDtypeStruct((rows, heads, HEAD_DIM), jnp.bfloat16),
        cost_estimate=pl.CostEstimate(
            flops=8 * rows * heads * positions * HEAD_DIM,
            bytes_accessed=4 * rows * positions * width,
            transcendentals=2 * rows * heads * positions,
        ),
    )(lengths, query, cache, own_key, own_value)
    return out.reshape(rows, heads * HEAD_DIM)


def weave_kernel(key_ref, value_ref, out_ref):
    tokens, width = key_ref.shape[2], key_ref.shape[3]
    part = 128
    row = lax.broadcasted_iota(jnp.int32, (2 * part, 2 * part), 0)
    column = lax.broadcasted_iota(jnp.int32, (2 * part, 2 * part), 1)
    order = jnp.where(column == (row % 2) * part + row // 2, 1.0, 0.0).astype(jnp.bfloat16)
    for at in range(0, tokens, part):
        both = jnp.concatenate(
            [key_ref[0, 0, at : at + part, :], value_ref[0, 0, at : at + part, :]], axis=0
        )
        woven = jnp.dot(order, both, preferred_element_type=jnp.float32).astype(jnp.bfloat16)
        out_ref[0, 0, at : at + part, :, :] = woven.reshape(part, 2, width)


def weave(keys, values):
    sources, slots, tokens, width = keys.shape
    spec = pl.BlockSpec((1, 1, tokens, width), lambda slot, source: (source, slot, 0, 0))
    return pl.pallas_call(
        weave_kernel,
        grid=(slots, sources),
        in_specs=[spec, spec],
        out_specs=pl.BlockSpec(
            (1, 1, tokens, 2, width), lambda slot, source: (0, slot, source, 0, 0)
        ),
        out_shape=jax.ShapeDtypeStruct((1, slots, sources * tokens, 2, width), jnp.bfloat16),
        cost_estimate=pl.CostEstimate(
            flops=1024 * slots * sources * tokens * width,
            bytes_accessed=8 * slots * sources * tokens * width,
            transcendentals=0,
        ),
    )(keys, values)


def slot_hits(owners, decoders):
    requests = owners.shape[0]
    order = jnp.arange(requests, dtype=jnp.int32)
    same = owners[:, None] == owners[None, :]
    slot_of = jnp.sum((same & (order[None, :] < order[:, None])).astype(jnp.int32), axis=1)
    slot_hit = slot_of[None, :] == jnp.arange(CAP, dtype=jnp.int32)[:, None]
    owner_hit = owners[None, :] == jnp.arange(decoders, dtype=jnp.int32)[:, None]
    return owner_hit[:, None, :] & slot_hit[None, :, :]


def hand_over(arrived, hits, after):
    if after is not None:
        arrived = lax.optimization_barrier((arrived, after))[0]
    outgoing = jnp.zeros(hits.shape[:2] + arrived.shape[1:], arrived.dtype)
    for request in range(arrived.shape[0]):
        outgoing = jnp.where(
            hits[:, :, request][:, :, None, None], arrived[request][None, None], outgoing
        )
    landed = lax.all_to_all(outgoing, "seq", split_axis=0, concat_axis=0, tiled=True)
    return landed, outgoing


def body(
    prompt,
    key_value_weight,
    adapter_down_weight,
    adapter_up_weight,
    request_adapter_index,
    destination,
    rotated_query,
    key_value_cache,
    current_key_value,
    cached_length,
    row_adapter_index,
    output_weight,
    output_down_weight,
    output_up_weight,
):
    requests, tok_dev, model_width = prompt.shape
    width = key_value_weight.shape[2]
    shard = key_value_weight.shape[0]
    decoders = lax.axis_size("seq")
    heads = lax.axis_size("head")
    columns = 2 * ADAPTER_RANK
    tokens = prompt.reshape(requests * tok_dev, model_width)

    share = requests // heads if requests % heads == 0 else requests
    mine = lax.axis_index("head") * share if share < requests else 0
    my_adapter = lax.dynamic_slice_in_dim(request_adapter_index, mine, share)
    column = jnp.arange(ADAPTER_COUNT * columns, dtype=jnp.int32)
    wanted = my_adapter[:, None] * columns + jnp.arange(columns, dtype=jnp.int32)[None, :]
    pick = (wanted.reshape(-1)[:, None] == column[None, :]).astype(jnp.bfloat16)
    down = lax.dot_general(
        pick, adapter_down_weight, (((1,), (1,)), ((), ())), preferred_element_type=jnp.float32
    ).astype(jnp.bfloat16)
    matrix = key_value_weight.reshape(shard, 2 * width)
    down_all, down_first = gathered(down, "seq")
    matrix = lax.optimization_barrier((matrix, down_first))[0]
    key_all, key_first = gathered(matrix[:, :width], "seq")
    value_all, _ = gathered(matrix[:, width:], "seq", key_all)
    key_all = key_all.reshape(model_width, width)
    value_all = value_all.reshape(model_width, width)
    rotated_query = lax.optimization_barrier((rotated_query, key_first))[0]

    attended = attend(rotated_query, key_value_cache, current_key_value, cached_length)
    attn_rows = gathered(attended, "seq")[0].reshape(-1, attended.shape[1])
    ranks = ADAPTER_COUNT * ADAPTER_RANK
    down_flat = output_down_weight.reshape(output_down_weight.shape[0], ranks)
    up_flat = output_up_weight.reshape(ranks, output_up_weight.shape[2])
    rank_owner = jnp.arange(ranks, dtype=jnp.int32) // ADAPTER_RANK
    low_rows = jnp.dot(attn_rows, down_flat, preferred_element_type=jnp.float32)
    low_rows = jnp.where(row_adapter_index[:, None] == rank_owner[None, :], low_rows, 0.0)
    terms = jnp.dot(attn_rows, output_weight, preferred_element_type=jnp.float32)
    terms = terms + jnp.dot(
        low_rows.astype(jnp.bfloat16), up_flat, preferred_element_type=jnp.float32
    )
    decoded = scattered_sum(terms, "head").astype(jnp.bfloat16)

    my_tokens = lax.dynamic_slice_in_dim(prompt, mine, share, axis=0)
    my_down = down_all.transpose(1, 0, 2).reshape(share, columns, model_width)
    my_low = jnp.einsum("rtk,rck->rct", my_tokens, my_down, preferred_element_type=jnp.float32)
    low = gathered(my_low, "head")[0] if share < requests else my_low[None]
    low = low.reshape(requests, 2, ADAPTER_RANK, tok_dev).astype(jnp.bfloat16)
    own = jnp.eye(requests, dtype=jnp.bool_)[None, :, None, :, None]
    spread = jnp.where(
        own, low.transpose(1, 0, 2, 3)[:, :, :, None, :], jnp.zeros((), jnp.bfloat16)
    ).reshape(2, requests * ADAPTER_RANK, requests * tok_dev)
    selector = request_adapter_index[:, None] == jnp.arange(ADAPTER_COUNT, dtype=jnp.int32)[None, :]
    up = jnp.einsum(
        "um,mdzt->duzt",
        selector.astype(jnp.bfloat16),
        adapter_up_weight,
        preferred_element_type=jnp.float32,
    ).astype(jnp.bfloat16)
    up = up.reshape(2, requests * ADAPTER_RANK, width)

    pool_index = lax.axis_index("pool")
    other_owners = lax.dynamic_slice_in_dim(destination, (1 - pool_index) * requests, requests)
    hits = slot_hits(other_owners, decoders)

    arrived = []
    for which, weight in enumerate((key_all, value_all)):
        base = jnp.dot(tokens, weight, preferred_element_type=jnp.float32)
        extra = lax.dot_general(
            spread[which], up[which], (((0,), (0,)), ((), ())), preferred_element_type=jnp.float32
        )
        block = (base + extra).astype(jnp.bfloat16).reshape(requests, tok_dev, width)
        arrived.append(exchanged(block, "pool", 1))
    handed, outgoing = [], block
    for blocks in arrived:
        landed, outgoing = hand_over(blocks, hits, outgoing)
        handed.append(landed)
    return (weave(handed[0], handed[1]), decoded)


def solution(mesh):
    in_specs = (
        P("pool", "seq", None),
        P("seq", None, "head"),
        P("seq", None),
        P(None, None, None, "head"),
        P("pool"),
        P(),
        P(("pool", "seq"), "head"),
        P(("pool", "seq"), None, None, "head"),
        P(("pool", "seq"), None, "head"),
        P(("pool", "seq")),
        P("pool"),
        P("head", "seq"),
        P("head", None, None),
        P(None, None, "seq"),
    )
    out_specs = (P(("pool", "seq"), None, None, None, "head"), P(("pool", "head"), "seq"))
    return jax.shard_map(body, mesh=mesh, in_specs=in_specs, out_specs=out_specs, check_vma=False)
```

profile of v0, /device:TPU:1, one launch (start us, length us, event | category | flops | bytes accessed | tf_op | source)
XLA Modules:
  0.0 192.5 jit_solution(15698170936103945559)
XLA Ops:
  3.0 2.1 %collective-permute-start = (bf16[1,32,2048]{2,1,0:T(8,128)(2,1)S(1)}, bf16[1,32,2048]{2,1,0:T(8,128)(2,1)S(1)}, u32[]{:S(2)}, u32[]{:S(2)}) collective-permute-start(bf16[1,32,2048]{2,1,0:T(8,128)(2,1)S(1)} %fusion.5), channel_id=1, source_target_pairs={{0,8},{4,12},{8,0},{12,4},{1,9},{5,13},{9,1},{13,5},{2,10},{6,14},... | collective-permute-start | bytes 393224 | tf_op jit(solution)/shard_map/ppermute | solution.py:16
  7.4 2.0 %copy.46 = bf16[256,8,2,256]{3,1,2,0:T(8,128)(2,1)S(1)} copy(bf16[256,8,2,256]{3,2,1,0:T(2,128)(2,1)} %bitcast.219) | data formatting | bytes 4194304
  10.7 1.4 slice_bitcast_fusion
  12.8 6.0 %fusion.8 = bf16[1,1,32,512]{3,2,1,0:T(8,128)(2,1)S(1)} fusion(bf16[32,8192]{1,0:T(8,128)(2,1)S(1)} %bitcast.216, bf16[4,512,8192]{2,1,0:T(8,128)(2,1)} %param.14, s32[]{:T(128)S(6)} %select_n.271), kind=kOutput, calls=%fused_computation.26 | convolution fusion | flops 268435456 | bytes 8945668 | tf_op jit(solution)/shard_map/rtk,rck->rct/dot_general | solution.py:241
  18.9 2.3 %collective-permute-start.4 = (bf16[1,1,32,512]{3,2,1,0:T(8,128)(2,1)S(1)}, bf16[1,1,32,512]{3,2,1,0:T(8,128)(2,1)S(1)}, u32[]{:S(2)}, u32[]{:S(2)}) collective-permute-start(bf16[1,1,32,512]{3,2,1,0:T(8,128)(2,1)S(1)} %fusion.8), channel_id=1, source_target_pairs={{0,2},{1,3},{2,0},{3,1},{4,6},{5,7},{6,4},{7,5},{8,10},{9,11},{10,... | collective-permute-start | bytes 98312 | tf_op jit(solution)/shard_map/ppermute | solution.py:16
  26.6 10.6 %collective-permute-done.1 = bf16[1,2048,256]{2,1,0:T(8,128)(2,1)} collective-permute-done((bf16[1,2048,256]{2,1,0:T(8,128)(2,1)}, bf16[1,2048,256]{2,1,0:T(8,128)(2,1)}, u32[]{:S(2)}, u32[]{:S(2)}) %collective-permute-start.1) | collective-permute-done | bytes 1048608 | tf_op jit(solution)/shard_map/ppermute | solution.py:16
  37.9 9.3 %shard_map.150 = bf16[48,16,128]{2,1,0:T(8,128)(2,1)} custom-call(s32[48]{0:T(128)} %lengths.1, bf16[48,16,128]{2,1,0:T(8,128)(2,1)} %bitcast.226, bf16[48,128,2,256]{3,2,1,0:T(2,128)(2,1)} %cache_ref.1, bf16[48,2,128]{2,1,0:T(2,128)(2,1)} %reshape_squeeze.6.key_ref, bf16[48,2,128]{2,1,0:T(2,128)(2,1)} %reshape_squeeze.7.value_ref), custom_call_target="tpu_custom_call" | custom-call | flops 100663296 | bytes 6291456 | tf_op jit(solution)/shard_map/pallas_call | solution.py:105
  48.7 1.5 select_bitcast_fusion.7
  50.4 1.7 collective-permute-start.2
  52.1 11.7 %collective-permute-done.10 = bf16[1,48,2048]{2,1,0:T(8,128)(2,1)S(1)} collective-permute-done((bf16[1,48,2048]{2,1,0:T(8,128)(2,1)S(1)}, bf16[1,48,2048]{2,1,0:T(8,128)(2,1)S(1)}, u32[]{:S(2)}, u32[]{:S(2)}) %collective-permute-start.10) | collective-permute-done | bytes 196640 | tf_op jit(solution)/shard_map/ppermute | solution.py:16
  66.4 3.1 %fusion.30 = f32[192,2048]{1,0:T(8,128)} fusion(bf16[192,2048]{1,0:T(8,128)(2,1)S(1)} %bitcast.214, bf16[2048,2048]{1,0:T(8,128)(2,1)S(1)} %bitcast.234), kind=kOutput, calls=%fused_computation.103 | convolution fusion | flops 1610612736 | bytes 10747904 | tf_op jit(solution)/shard_map/dot_general | solution.py:233
  69.7 2.4 %pad_maximum_fusion = bf16[2,2,2048,256]{3,2,1,0:T(8,128)(2,1)} fusion(bf16[2,1,2048,256]{3,2,1,0:T(8,128)(2,1)S(1)} %get-tuple-element.19, bf16[2,1,2048,256]{3,2,1,0:T(8,128)(2,1)S(1)} %get-tuple-element.18), kind=kLoop, calls=%fused_computation.3 | loop fusion | flops 2097152 | bytes 8388608 | tf_op jit(solution)/shard_map/stack | solution.py:33
  72.1 1.4 select_bitcast_fusion.5
  73.5 1.8 maximum_bitcast_fusion.1
  75.6 17.0 %convolution_bitcast_fusion.1 = f32[2048,256]{0,1:T(8,128)} fusion(bf16[8192,256]{1,0:T(8,128)(2,1)} %bitcast.212, bf16[2048,8192]{1,0:T(8,128)(2,1)} %bitcast.217), kind=kOutput, calls=%fused_computation.8 | convolution fusion | flops 8589934592 | bytes 39845888 | tf_op jit(solution)/shard_map/dot_general | solution.py:263
  92.6 2.2 %fusion.3 = bf16[2048,256]{0,1:T(8,128)(2,1)S(1)} fusion(f32[2048,256]{0,1:T(8,128)} %convolution_bitcast_fusion.1, bf16[64,2048]{1,0:T(8,128)(2,1)S(1)} %bitcast.225, bf16[64,256]{1,0:T(8,128)(2,1)S(1)} %bitcast.232), kind=kOutput, calls=%fused_computation.9 | convolution fusion | flops 68157440 | bytes 3440640 | tf_op jit(solution)/shard_map/dot_general | solution.py:264
  97.3 1.9 select_bitcast_fusion.1
  99.6 2.3 %copy.32 = bf16[2,2,2048,256]{3,2,1,0:T(8,128)(2,1)} copy(bf16[2,2,2048,256]{3,2,0,1:T(8,128)(2,1)S(1)} %pad_maximum_fusion.1) | data formatting | bytes 8388608 | tf_op jit(solution)/shard_map/stack | solution.py:33
  101.9 15.4 %convolution_bitcast_fusion = f32[2048,256]{0,1:T(8,128)S(1)} fusion(bf16[8192,256]{1,0:T(8,128)(2,1)} %bitcast.213, bf16[2048,8192]{1,0:T(8,128)(2,1)} %bitcast.218), kind=kOutput, calls=%fused_computation.6 | convolution fusion | flops 8589934592 | bytes 39845888 | tf_op jit(solution)/shard_map/dot_general | solution.py:263
  118.5 1.6 copy.35
  122.2 1.8 select_select_fusion.1
  124.1 5.8 %all-to-all-start = ((bf16[4,2,512,256]{3,2,1,0:T(8,128)(2,1)}), bf16[4,2,512,256]{3,2,1,0:T(8,128)(2,1)}, u32[]{:S(2)}, u32[]{:S(2)}) async-start(bf16[4,2,512,256]{3,2,1,0:T(8,128)(2,1)} %select_select_fusion.1), calls=%async_computation | async-start | bytes 4194304 | tf_op jit(solution)/shard_map/all_to_all | solution.py:179
  129.9 2.6 %convolution_add_fusion.2 = f32[192,2048]{1,0:T(8,128)S(1)} fusion(f32[192,2048]{1,0:T(8,128)} %fusion.30, bf16[128,2048]{1,0:T(8,128)(2,1)S(1)} %bitcast.227, bf16[192,2048]{1,0:T(8,128)(2,1)S(1)} %bitcast.215, bf16[2048,128]{0,1:T(8,128)(2,1)} %bitcast.228, s32[128]{0:T(128)S(1)} %copy-done.10, s32[192]{0:T(256)S(1)} %copy-done.9), kind=kOutput, calls=%fused_computation.11 | convolution fusion | flops 201793536 | bytes 4982016 | tf_op jit(solution)/shard_map/dot_general | solution.py:234
  132.6 1.4 collective-permute-start.12
  134.0 11.1 %collective-permute-done.9 = bf16[4,512,256]{2,1,0:T(8,128)(2,1)} collective-permute-done((bf16[4,512,256]{2,1,0:T(8,128)(2,1)}, bf16[4,512,256]{2,1,0:T(8,128)(2,1)}, u32[]{:S(2)}, u32[]{:S(2)}) %collective-permute-start.9) | collective-permute-done | bytes 1048608 | tf_op jit(solution)/shard_map/ppermute | solution.py:16
  146.3 1.9 select_select_fusion
  148.2 6.5 %all-to-all-done.key_ref = bf16[4,2,512,256]{3,2,1,0:T(8,128)(2,1)} async-done(((bf16[4,2,512,256]{3,2,1,0:T(8,128)(2,1)}), bf16[4,2,512,256]{3,2,1,0:T(8,128)(2,1)}, u32[]{:S(2)}, u32[]{:S(2)}) %all-to-all-start) | async-done | bytes 2097184 | tf_op jit(solution)/shard_map/all_to_all | solution.py:179
  154.7 5.4 %all-to-all-start.1 = ((bf16[4,2,512,256]{3,2,1,0:T(8,128)(2,1)}), bf16[4,2,512,256]{3,2,1,0:T(8,128)(2,1)}, u32[]{:S(2)}, u32[]{:S(2)}) async-start(bf16[4,2,512,256]{3,2,1,0:T(8,128)(2,1)} %select_select_fusion), calls=%async_computation.1 | async-start | bytes 4194304 | tf_op jit(solution)/shard_map/all_to_all | solution.py:179
  161.4 2.4 %collective-permute-start.13 = (f32[1,48,2048]{2,1,0:T(8,128)S(1)}, f32[1,48,2048]{2,1,0:T(8,128)S(1)}, u32[]{:S(2)}, u32[]{:S(2)}) collective-permute-start(f32[1,48,2048]{2,1,0:T(8,128)S(1)} %select_bitcast_fusion.9), channel_id=1, source_target_pairs={{0,2},{1,3},{2,0},{3,1},{4,6},{5,7},{6,4},{7,5},{8,10},{9,11},{10,... | collective-permute-start | bytes 1179656 | tf_op jit(solution)/shard_map/ppermute | solution.py:16
  163.8 17.6 %collective-permute-done.13 = f32[1,48,2048]{2,1,0:T(8,128)S(1)} collective-permute-done((f32[1,48,2048]{2,1,0:T(8,128)S(1)}, f32[1,48,2048]{2,1,0:T(8,128)S(1)}, u32[]{:S(2)}, u32[]{:S(2)}) %collective-permute-start.13) | collective-permute-done | bytes 393248 | tf_op jit(solution)/shard_map/ppermute | solution.py:16
  182.2 2.7 %all-to-all-done.1.value_ref = bf16[4,2,512,256]{3,2,1,0:T(8,128)(2,1)} async-done(((bf16[4,2,512,256]{3,2,1,0:T(8,128)(2,1)}), bf16[4,2,512,256]{3,2,1,0:T(8,128)(2,1)}, u32[]{:S(2)}, u32[]{:S(2)}) %all-to-all-start.1) | async-done | bytes 2097184 | tf_op jit(solution)/shard_map/all_to_all | solution.py:179
  184.9 7.6 %shard_map.149 = bf16[1,2,2048,2,256]{4,3,2,1,0:T(2,128)(2,1)} custom-call(bf16[4,2,512,256]{3,2,1,0:T(8,128)(2,1)} %all-to-all-done.key_ref, bf16[4,2,512,256]{3,2,1,0:T(8,128)(2,1)} %all-to-all-done.1.value_ref), custom_call_target="tpu_custom_call" | custom-call | flops 1073741824 | bytes 8388608 | tf_op jit(solution)/shard_map/pallas_call | solution.py:145
  (99 shorter events, 26.6 us)
Async XLA Ops:
  0.6 2.0 %copy-start = (bf16[2048,256]{1,0:T(8,128)(2,1)S(1)}, bf16[2048,256]{1,0:T(8,128)(2,1)}, u32[]{:S(2)}) copy-start(bf16[2048,256]{1,0:T(8,128)(2,1)} %param.16) | copy-start | bytes 3145732
  3.0 6.6 %collective-permute-start = (bf16[1,32,2048]{2,1,0:T(8,128)(2,1)S(1)}, bf16[1,32,2048]{2,1,0:T(8,128)(2,1)S(1)}, u32[]{:S(2)}, u32[]{:S(2)}) collective-permute-start(bf16[1,32,2048]{2,1,0:T(8,128)(2,1)S(1)} %fusion.5), channel_id=1, source_target_pairs={{0,8},{4,12},{8,0},{12,4},{1,9},{5,13},{9,1},{13,5},{2,10},{6,14},... | collective-permute-start | bytes 393224 | tf_op jit(solution)/shard_map/ppermute | solution.py:16
  7.4 2.1 %copy-start.8 = (bf16[48,2,256]{2,1,0:T(2,128)(2,1)S(1)}, bf16[48,2,256]{2,1,0:T(2,128)(2,1)}, u32[]{:S(2)}) copy-start(bf16[48,2,256]{2,1,0:T(2,128)(2,1)} %param.22) | copy-start | bytes 147460
  9.7 2.9 %collective-permute-start.3 = (bf16[2,32,2048]{2,1,0:T(8,128)(2,1)S(1)}, bf16[2,32,2048]{2,1,0:T(8,128)(2,1)S(1)}, u32[]{:S(2)}, u32[]{:S(2)}) collective-permute-start(bf16[2,32,2048]{2,1,0:T(8,128)(2,1)S(1)} %maximum_bitcast_fusion.3), channel_id=1, source_target_pairs={{0,4},{4,0},{8,12},{12,8},{1,5},{5,1},{9,13},{13,9},{2,6},{6,2},{1... | collective-permute-start | bytes 786440 | tf_op jit(solution)/shard_map/ppermute | solution.py:16
  12.2 25.0 %collective-permute-start.1 = (bf16[1,2048,256]{2,1,0:T(8,128)(2,1)}, bf16[1,2048,256]{2,1,0:T(8,128)(2,1)}, u32[]{:S(2)}, u32[]{:S(2)}) collective-permute-start(bf16[1,2048,256]{2,1,0:T(8,128)(2,1)} %get-tuple-element.25), channel_id=1, source_target_pairs={{0,8},{4,12},{8,0},{12,4},{1,9},{5,13},{9,1},{13,5},{2,10},{6,14},... | collective-permute-start | bytes 3145736 | tf_op jit(solution)/shard_map/ppermute | solution.py:16
  12.8 24.4 %copy-start.7 = (bf16[48,2048]{1,0:T(8,128)(2,1)S(1)}, bf16[48,2048]{1,0:T(8,128)(2,1)}, u32[]{:S(2)}) copy-start(bf16[48,2048]{1,0:T(8,128)(2,1)} %param.20) | copy-start | bytes 589828
  18.9 4.1 %collective-permute-start.4 = (bf16[1,1,32,512]{3,2,1,0:T(8,128)(2,1)S(1)}, bf16[1,1,32,512]{3,2,1,0:T(8,128)(2,1)S(1)}, u32[]{:S(2)}, u32[]{:S(2)}) collective-permute-start(bf16[1,1,32,512]{3,2,1,0:T(8,128)(2,1)S(1)} %fusion.8), channel_id=1, source_target_pairs={{0,2},{1,3},{2,0},{3,1},{4,6},{5,7},{6,4},{7,5},{8,10},{9,11},{10,... | collective-permute-start | bytes 98312 | tf_op jit(solution)/shard_map/ppermute | solution.py:16
  23.0 3.6 %collective-permute-start.5 = (bf16[2,1,32,512]{3,2,0,1:T(8,128)(2,1)S(1)}, bf16[2,1,32,512]{3,2,0,1:T(8,128)(2,1)S(1)}, u32[]{:S(2)}, u32[]{:S(2)}) collective-permute-start(bf16[2,1,32,512]{3,2,0,1:T(8,128)(2,1)S(1)} %maximum_bitcast_fusion.4), channel_id=1, source_target_pairs={{0,1},{1,0},{2,3},{3,2},{4,5},{5,4},{6,7},{7,6},{8,9},{9,8},{10,11... | collective-permute-start | bytes 196616 | tf_op jit(solution)/shard_map/ppermute | solution.py:16
  25.0 47.1 %collective-permute-start.7 = (bf16[1,2048,256]{2,1,0:T(8,128)(2,1)}, bf16[1,2048,256]{2,1,0:T(8,128)(2,1)}, u32[]{:S(2)}, u32[]{:S(2)}) collective-permute-start(bf16[1,2048,256]{2,1,0:T(8,128)(2,1)} %get-tuple-element.24), channel_id=1, source_target_pairs={{0,8},{4,12},{8,0},{12,4},{1,9},{5,13},{9,1},{13,5},{2,10},{6,14},... | collective-permute-start | bytes 3145736 | tf_op jit(solution)/shard_map/ppermute | solution.py:16
  48.2 15.6 %collective-permute-start.10 = (bf16[1,48,2048]{2,1,0:T(8,128)(2,1)S(1)}, bf16[1,48,2048]{2,1,0:T(8,128)(2,1)S(1)}, u32[]{:S(2)}, u32[]{:S(2)}) collective-permute-start(bf16[1,48,2048]{2,1,0:T(8,128)(2,1)S(1)} %broadcast_in_dim_reshape.4), channel_id=1, source_target_pairs={{0,8},{4,12},{8,0},{12,4},{1,9},{5,13},{9,1},{13,5},{2,10},{6,14},... | collective-permute-start | bytes 589832 | tf_op jit(solution)/shard_map/ppermute | solution.py:16
  48.7 17.6 %slice-start = ((s8[8388608]{0:T(1024)(128)(4,1)}), s8[4194304]{0:T(1024)(128)(4,1)S(1)}, s32[]{:S(2)}) async-start(s8[8388608]{0:T(1024)(128)(4,1)} %bitcast.233), calls=%async_computation.2 | async-start | bytes 8388608
  50.2 14.6 %copy-start.11 = (pred[4,4]{1,0:T(4,128)(4,1)S(1)}, pred[4,4]{1,0:T(4,128)(4,1)}, u32[]{:S(2)}) copy-start(pred[4,4]{1,0:T(4,128)(4,1)} %iota_compare_fusion.3) | copy-start | bytes 52
  50.2 16.1 %slice-start.1 = ((s8[8388608]{0:T(1024)(128)(4,1)}), s8[4194304]{0:T(1024)(128)(4,1)S(1)}, s32[]{:S(2)}) async-start(s8[8388608]{0:T(1024)(128)(4,1)} %bitcast.233), calls=%async_computation.3 | async-start | bytes 8388608
  50.4 19.0 %collective-permute-start.2 = (bf16[2,2048,256]{2,1,0:T(8,128)(2,1)S(1)}, bf16[2,2048,256]{2,1,0:T(8,128)(2,1)S(1)}, u32[]{:S(2)}, u32[]{:S(2)}) collective-permute-start(bf16[2,2048,256]{2,1,0:T(8,128)(2,1)S(1)} %maximum_bitcast_fusion), channel_id=1, source_target_pairs={{0,4},{4,0},{8,12},{12,8},{1,5},{5,1},{9,13},{13,9},{2,6},{6,2},{1... | collective-permute-start | bytes 6291464 | tf_op jit(solution)/shard_map/ppermute | solution.py:16
  63.9 2.3 %collective-permute-start.11 = (bf16[2,48,2048]{2,1,0:T(8,128)(2,1)S(1)}, bf16[2,48,2048]{2,1,0:T(8,128)(2,1)S(1)}, u32[]{:S(2)}, u32[]{:S(2)}) collective-permute-start(bf16[2,48,2048]{2,1,0:T(8,128)(2,1)S(1)} %maximum_bitcast_fusion.2), channel_id=1, source_target_pairs={{0,4},{4,0},{8,12},{12,8},{1,5},{5,1},{9,13},{13,9},{2,6},{6,2},{1... | collective-permute-start | bytes 1179656 | tf_op jit(solution)/shard_map/ppermute | solution.py:16
  66.3 3.1 %copy-start.4 = (bf16[2,2,48,2048]{3,2,1,0:T(8,128)(2,1)}, bf16[2,2,48,2048]{3,2,1,0:T(8,128)(2,1)S(1)}, u32[]{:S(2)}) copy-start(bf16[2,2,48,2048]{3,2,1,0:T(8,128)(2,1)S(1)} %pad_maximum_fusion.2) | copy-start | bytes 2359300
  73.5 1.8 copy-start.2
  75.2 22.1 %collective-permute-start.8 = (bf16[2,2048,256]{2,1,0:T(8,128)(2,1)}, bf16[2,2048,256]{2,1,0:T(8,128)(2,1)}, u32[]{:S(2)}, u32[]{:S(2)}) collective-permute-start(bf16[2,2048,256]{2,1,0:T(8,128)(2,1)} %maximum_bitcast_fusion.1), channel_id=1, source_target_pairs={{0,4},{4,0},{8,12},{12,8},{1,5},{5,1},{9,13},{13,9},{2,6},{6,2},{1... | collective-permute-start | bytes 6291464 | tf_op jit(solution)/shard_map/ppermute | solution.py:16
  92.6 4.7 %copy-start.3 = (bf16[1,1,2048,256]{3,2,1,0:T(8,128)(2,1)S(1)}, bf16[1,1,2048,256]{3,2,1,0:T(8,128)(2,1)}, u32[]{:S(2)}) copy-start(bf16[1,1,2048,256]{3,2,1,0:T(8,128)(2,1)} %copy-done.2) | copy-start | bytes 3145732
  96.1 24.8 %collective-permute-start.6 = (bf16[4,512,256]{2,1,0:T(8,128)(2,1)}, bf16[4,512,256]{2,1,0:T(8,128)(2,1)S(1)}, u32[]{:S(2)}, u32[]{:S(2)}) collective-permute-start(bf16[4,512,256]{2,1,0:T(8,128)(2,1)} %bitcast.221), channel_id=1, source_target_pairs={{0,16},{16,0},{1,17},{17,1},{2,18},{18,2},{3,19},{19,3},{4,20},{20... | collective-permute-start | bytes 3145736 | tf_op jit(solution)/shard_map/ppermute | solution.py:16
  121.0 24.1 %collective-permute-start.9 = (bf16[4,512,256]{2,1,0:T(8,128)(2,1)}, bf16[4,512,256]{2,1,0:T(8,128)(2,1)}, u32[]{:S(2)}, u32[]{:S(2)}) collective-permute-start(bf16[4,512,256]{2,1,0:T(8,128)(2,1)} %copy.35), channel_id=1, source_target_pairs={{0,16},{16,0},{1,17},{17,1},{2,18},{18,2},{3,19},{19,3},{4,20},{20... | collective-permute-start | bytes 3145736 | tf_op jit(solution)/shard_map/ppermute | solution.py:16
  124.1 5.8 %copy-start.5 = (bf16[2,2,48,2048]{3,2,1,0:T(8,128)(2,1)S(1)}, bf16[2,2,48,2048]{3,2,1,0:T(8,128)(2,1)}, u32[]{:S(2)}) copy-start(bf16[2,2,48,2048]{3,2,1,0:T(8,128)(2,1)} %copy-done.4) | copy-start | bytes 2359300
  124.1 5.8 %copy-start.6 = (bf16[8,16,2048]{2,1,0:T(8,128)(2,1)S(1)}, bf16[8,16,2048]{2,1,0:T(8,128)(2,1)}, u32[]{:S(2)}) copy-start(bf16[8,16,2048]{2,1,0:T(8,128)(2,1)} %param.27) | copy-start | bytes 1572868
  124.1 5.8 %copy-start.9 = (s32[192]{0:T(256)S(1)}, s32[192]{0:T(256)}, u32[]{:S(2)}) copy-start(s32[192]{0:T(256)} %param.24) | copy-start | bytes 2308
  124.1 5.8 %copy-start.10 = (s32[128]{0:T(128)S(1)}, s32[128]{0:T(128)}, u32[]{:S(2)}) copy-start(s32[128]{0:T(128)} %and_select_fusion) | copy-start | bytes 1540
  124.1 30.6 %all-to-all-start = ((bf16[4,2,512,256]{3,2,1,0:T(8,128)(2,1)}), bf16[4,2,512,256]{3,2,1,0:T(8,128)(2,1)}, u32[]{:S(2)}, u32[]{:S(2)}) async-start(bf16[4,2,512,256]{3,2,1,0:T(8,128)(2,1)} %select_select_fusion.1), calls=%async_computation | async-start | bytes 4194304 | tf_op jit(solution)/shard_map/all_to_all | solution.py:179
  132.6 27.5 %collective-permute-start.12 = (f32[2,48,2048]{2,1,0:T(8,128)S(1)}, f32[2,48,2048]{2,1,0:T(8,128)}, u32[]{:S(2)}, u32[]{:S(2)}) collective-permute-start(f32[2,48,2048]{2,1,0:T(8,128)S(1)} %select_bitcast_fusion.8), channel_id=1, source_target_pairs={{0,1},{1,0},{2,3},{3,2},{4,5},{5,4},{6,7},{7,6},{8,9},{9,8},{10,11... | collective-permute-start | bytes 2359304 | tf_op jit(solution)/shard_map/ppermute | solution.py:16
  154.7 30.2 %all-to-all-start.1 = ((bf16[4,2,512,256]{3,2,1,0:T(8,128)(2,1)}), bf16[4,2,512,256]{3,2,1,0:T(8,128)(2,1)}, u32[]{:S(2)}, u32[]{:S(2)}) async-start(bf16[4,2,512,256]{3,2,1,0:T(8,128)(2,1)} %select_select_fusion), calls=%async_computation.1 | async-start | bytes 4194304 | tf_op jit(solution)/shard_map/all_to_all | solution.py:179
  161.4 20.0 %collective-permute-start.13 = (f32[1,48,2048]{2,1,0:T(8,128)S(1)}, f32[1,48,2048]{2,1,0:T(8,128)S(1)}, u32[]{:S(2)}, u32[]{:S(2)}) collective-permute-start(f32[1,48,2048]{2,1,0:T(8,128)S(1)} %select_bitcast_fusion.9), channel_id=1, source_target_pairs={{0,2},{1,3},{2,0},{3,1},{4,6},{5,7},{6,4},{7,5},{8,10},{9,11},{10,... | collective-permute-start | bytes 1179656 | tf_op jit(solution)/shard_map/ppermute | solution.py:16
  184.9 7.6 %copy-start.1 = (bf16[2048,256]{1,0:T(8,128)(2,1)S(1)}, bf16[2048,256]{1,0:T(8,128)(2,1)}, u32[]{:S(2)}) copy-start(bf16[2048,256]{1,0:T(8,128)(2,1)} %param.16) | copy-start | bytes 3145732
where the time goes:
time: 194 us; the launch traced here: 193 us
  waiting for transfers between devices  62.3 us (32%)
  matrix products  48.2 us (25%)
  starting transfers between devices  29.2 us (15%)
  other arithmetic  17.7 us (9%)
  Pallas kernels  16.9 us (9%)
  local copies, waits for them, and re-layouts  16.5 us (9%)
    ppermute x14, waiting for transfers between devices, exchanged(): return lax.ppermute(value, axis, pairs)  53.1 us
    dot_general x2, matrix products, body(): base = jnp.dot(tokens, weight, preferred_element_type=jnp.float32)  32.4 us
    ppermute x14, starting transfers between devices, exchanged(): return lax.ppermute(value, axis, pairs)  18 us
    all_to_all x2, starting transfers between devices, hand_over(): lax.all_to_all(outgoing, 'seq', split_axis=0, concat_axis=0, tiled=True)  11.2 us
    pallas_call x1, Pallas kernels, attend(): pl.pallas_call(attend_kernel, grid_spec=pltpu.PrefetchScalarGridSpec(num_...  9.27 us
    all_to_all x2, waiting for transfers between devices, hand_over(): lax.all_to_all(outgoing, 'seq', split_axis=0, concat_axis=0, tiled=True)  9.21 us
    another operation x15, other arithmetic, gathered(): held = jnp.stack([first, second], axis=1).reshape((-1,) + value.shape)  8.12 us
    pallas_call x1, Pallas kernels, weave(): pl.pallas_call(weave_kernel, grid=(slots, sources), in_specs=[spec, spec]...  7.61 us
  transfers between devices with their start and end apart: 16, of which 9 were waited for; matrix products, arithmetic and copies ran while one was open for 40% of the time, Pallas kernels for 5%

commit v1 on v0

--- a/solution.py
+++ b/solution.py
@@ -273,6 +273,605 @@
     return (weave(handed[0], handed[1]), decoded)
 
 
+MESH = pl.DeviceIdType.MESH
+PIECES = 4
+SLOTS = 3
+TILE = 256
+PART = 128
+
+
+def serve_kernel(
+    dest_ref,
+    adapter_ref,
+    length_ref,
+    prompt_ref,
+    wa_ref,
+    wb_ref,
+    down_ref,
+    up_ref,
+    query_ref,
+    cache_ref,
+    current_ref,
+    keep_ref,
+    ow_ref,
+    odown_ref,
+    oup_ref,
+    out_ref,
+    decoded_ref,
+    w0,
+    w1,
+    pbuf,
+    acc,
+    cbuf,
+    owbuf,
+    qbuf,
+    abuf,
+    att_all,
+    down_all,
+    low_acc,
+    low_all,
+    terms,
+    tsend,
+    trecv,
+    hsend,
+    recvx0,
+    recvx1,
+    sibx0,
+    sibx1,
+    ysend,
+    yrecv0,
+    yrecv1,
+    siby0,
+    siby1,
+    ssem,
+    rsem,
+    lsem,
+):
+    f32, bf16 = jnp.float32, jnp.bfloat16
+    requests, tok, model = prompt_ref.shape
+    shard = wa_ref.shape[0]
+    half_width = 2 * shard
+    heads = lax.axis_size("head")
+    rows = query_ref.shape[0]
+    q_heads = query_ref.shape[1] // HEAD_DIM
+    columns = 2 * ADAPTER_RANK
+    p, me, h = lax.axis_index("pool"), lax.axis_index("seq"), lax.axis_index("head")
+    y, c = me // 2, me % 2
+    sib, peer, far = y * 2 + 1 - c, (1 - y) * 2 + c, (1 - y) * 2 + 1 - c
+    slots = requests - 1
+    recvx, sibx = (recvx0, recvx1), (sibx0, sibx1)
+    yrecv, siby = (yrecv0, yrecv1), (siby0, siby1)
+    w = (w0, w1)
+
+    names = {}
+
+    def sem_of(name, index=0):
+        if name not in names:
+            raise KeyError(name)
+        return names[name] + index
+
+    at = 0
+    for name, count in (
+        ("ya", PIECES), ("xa", PIECES), ("sa", 1), ("fa", 2), ("yb", 2), ("sb", 1), ("fb", 2),
+        ("yd", 1), ("sd", 1), ("fd", 1), ("yt", 1), ("st", 1), ("ft", 1),
+        ("zl", heads - 1), ("zt", heads - 1),
+        ("hx", 2 * requests), ("hs", 2 * requests), ("hy", 2 * slots), ("hf", 2 * slots),
+    ):
+        names[name] = at
+        at += count
+
+    sent = []
+
+    def remote(src, dst, name, index, target):
+        i = sem_of(name, index)
+        return pltpu.make_async_remote_copy(
+            src_ref=src, dst_ref=dst, send_sem=ssem.at[i], recv_sem=rsem.at[i],
+            device_id=target, device_id_type=MESH,
+        )
+
+    def send(src, dst, name, index, target, keep=True):
+        copy = remote(src, dst, name, index, target)
+        copy.start()
+        if keep:
+            sent.append(copy)
+
+    def arrive(dst, name, index, target):
+        remote(dst, dst, name, index, target).wait_recv()
+
+    to_sib, to_peer, to_x = {"seq": sib}, {"seq": peer}, {"pool": 1 - p}
+
+    def rows_of(ref, start, size):
+        return ref.at[pl.ds(pl.multiple_of(start, PART), size)]
+
+    barrier = pltpu.get_barrier_semaphore()
+    partners = [to_sib, to_peer, to_x] + [{"head": (h + k) % heads} for k in range(1, heads)]
+    for partner in partners:
+        pl.semaphore_signal(barrier, inc=1, device_id=partner, device_id_type=MESH)
+    pl.semaphore_wait(barrier, len(partners))
+
+    piece = shard // (2 * PIECES)
+
+    def y_piece(k):
+        row = (p * PIECES + k) * piece
+        send(rows_of(wa_ref, row, piece), rows_of(w0, me * shard + row, piece), "ya", k, to_peer)
+
+    def y_arrived(k):
+        row = peer * shard + (p * PIECES + k) * piece
+        arrive(rows_of(w0, row, piece), "ya", k, to_peer)
+        send(rows_of(w0, row, piece), rows_of(w0, row, piece), "xa", k, to_x)
+
+    def x_arrived(k):
+        row = peer * shard + ((1 - p) * PIECES + k) * piece
+        arrive(rows_of(w0, row, piece), "xa", k, to_x)
+
+    def prompt_load(step):
+        if isinstance(step, int) and step < 2:
+            r, half = h, (y if step == 0 else 1 - y)
+        else:
+            t = step - 2
+            r, turn = t % requests, (t // requests) % 2
+            half = turn + y - 2 * turn * y
+        slot = step % SLOTS
+        return pltpu.make_async_copy(
+            prompt_ref.at[r, :, pl.ds(pl.multiple_of(half * half_width, half_width), half_width)],
+            pbuf.at[slot],
+            lsem.at[slot],
+        )
+
+    total_steps = 2 + 4 * requests
+    y_piece(0)
+    y_piece(1)
+    cache_copy = pltpu.make_async_copy(cache_ref, cbuf, lsem.at[SLOTS])
+    cache_copy.start()
+    own_a = pltpu.make_async_copy(wa_ref, rows_of(w0, me * shard, shard), lsem.at[SLOTS + 1])
+    own_b = pltpu.make_async_copy(wb_ref, rows_of(w1, me * shard, shard), lsem.at[SLOTS + 2])
+    own_a.start()
+    send(wa_ref, rows_of(w0, me * shard, shard), "sa", 0, to_sib)
+
+    pick_row = lax.broadcasted_iota(jnp.int32, (columns, down_ref.shape[1]), 0)
+    pick_col = lax.broadcasted_iota(jnp.int32, (columns, down_ref.shape[1]), 1)
+    pick = jnp.where(pick_col == pick_row + adapter_ref[h] * columns, 1.0, 0.0).astype(bf16)
+    my_cols = pl.ds(pl.multiple_of(me * shard, shard), shard)
+    down_all[:, my_cols] = lax.dot_general(
+        pick, down_ref[...], (((1,), (1,)), ((), ())), preferred_element_type=f32
+    ).astype(bf16)
+    for step in range(SLOTS):
+        prompt_load(step).start()
+    own_b.start()
+
+    def ow_load(n):
+        width = owbuf.shape[2]
+        return pltpu.make_async_copy(
+            ow_ref.at[:, pl.ds(pl.multiple_of(n * width, width), width)],
+            owbuf.at[n % 2],
+            lsem.at[SLOTS + 3 + n % 2],
+        )
+
+    for head in range(q_heads):
+        qbuf[pl.ds(head, rows, stride=q_heads), :] = query_ref[
+            :, head * HEAD_DIM : (head + 1) * HEAD_DIM
+        ].astype(f32)
+    down_view = down_all.at[:, my_cols]
+    send(down_view, down_view, "yd", 0, to_peer)
+    send(down_view, down_view, "sd", 0, to_sib)
+    y_piece(2)
+    y_piece(3)
+    send(wb_ref, rows_of(w1, me * shard, shard), "sb", 0, to_sib)
+    ow_load(0).start()
+    ow_load(1).start()
+    cache_copy.wait()
+
+    positions = cache_ref.shape[1]
+    kv_heads = current_ref.shape[2] // HEAD_DIM
+    groups = q_heads // kv_heads
+    batch = 8
+    factor = HEAD_DIM ** (-0.5)
+    lane = lax.broadcasted_iota(jnp.int32, (groups, 2 * positions), 1)
+
+    def attend_step(step):
+        start = step * batch
+        blocks, scores, owns, values = [], [], [], []
+        for row in range(batch):
+            pairs = cbuf[start + row].reshape(2 * positions, kv_heads * HEAD_DIM)
+            valid = (lane % 2 == 0) & (lane < 2 * length_ref[start + row])
+            now = current_ref[start + row].astype(f32)
+            for head in range(kv_heads):
+                span = slice(head * HEAD_DIM, (head + 1) * HEAD_DIM)
+                block = pairs[:, span]
+                query = qbuf[
+                    pl.ds(pl.multiple_of((start + row) * q_heads + head * groups, groups), groups), :
+                ]
+                own = jnp.sum(query * now[0:1, span], axis=1, keepdims=True) * factor
+                score = lax.dot_general(
+                    query.astype(bf16), block, (((1,), (1,)), ((), ())), preferred_element_type=f32
+                )
+                blocks.append(block)
+                scores.append(jnp.where(valid, score * factor, -1e30))
+                owns.append(own)
+                values.append(now[1:2, span])
+        score = jnp.concatenate(scores, axis=0)
+        own = jnp.concatenate(owns, axis=0)
+        highest = jnp.maximum(jnp.max(score, axis=1, keepdims=True), own)
+        raw = jnp.where(score > -1e29, jnp.exp(score - highest), 0.0)
+        own_raw = jnp.exp(own - highest)
+        normer = jnp.sum(raw, axis=1, keepdims=True) + own_raw
+        weights = pltpu.roll(raw / normer, 1, 1).astype(bf16)
+        own_weight = (own_raw / normer).astype(bf16).astype(f32)
+        for item in range(batch * kv_heads):
+            at_row = item * groups
+            mixed = jnp.dot(
+                weights[at_row : at_row + groups], blocks[item], preferred_element_type=f32
+            )
+            abuf[
+                pl.ds(pl.multiple_of(start * q_heads + at_row, groups), groups), :
+            ] = mixed + own_weight[at_row : at_row + groups] * values[item]
+
+    batches = rows // batch
+    per = -(-batches // (PIECES - 1))
+    for k in range(PIECES - 1):
+        first, last = k * per, min(batches, (k + 1) * per)
+        if first < last:
+            pl.loop(first, last)(attend_step)
+        y_arrived(k)
+
+    for head in range(q_heads):
+        att_all[me, :, head * HEAD_DIM : (head + 1) * HEAD_DIM] = abuf[
+            pl.ds(head, rows, stride=q_heads), :
+        ].astype(bf16)
+    send(att_all.at[me], att_all.at[me], "yt", 0, to_peer)
+    send(att_all.at[me], att_all.at[me], "st", 0, to_sib)
+    half_shard = shard // 2
+    for k in range(2):
+        send(
+            rows_of(wb_ref, k * half_shard, half_shard),
+            rows_of(w1, me * shard + k * half_shard, half_shard), "yb", k, to_peer,
+        )
+    y_arrived(PIECES - 1)
+    peer_part = rows_of(w0, peer * shard + p * half_shard, half_shard)
+    send(peer_part, peer_part, "fa", 0, to_sib)
+
+    def cols_at(who):
+        return down_all.at[:, pl.ds(pl.multiple_of(who * shard, shard), shard)]
+
+    arrive(cols_at(peer), "yd", 0, to_peer)
+    send(cols_at(peer), cols_at(peer), "fd", 0, to_sib)
+    arrive(cols_at(sib), "sd", 0, to_sib)
+    arrive(cols_at(far), "fd", 0, to_sib)
+
+    tiles = tok // TILE
+    for step in range(2):
+        prompt_load(step).wait()
+        half = y if step == 0 else 1 - y
+        cols = pl.ds(pl.multiple_of(half * half_width, half_width), half_width)
+
+        @pl.loop(0, tiles)
+        def _(i):
+            at_row = pl.ds(pl.multiple_of(i * TILE, TILE), TILE)
+            part = lax.dot_general(
+                pbuf[step, at_row, :], down_all[:, cols], (((1,), (1,)), ((), ())),
+                preferred_element_type=f32,
+            )
+            if step == 0:
+                low_acc[at_row, :] = part
+            else:
+                low = jnp.concatenate(
+                    [low_acc[at_row, :] + part, jnp.zeros((TILE, PART - columns), f32)], axis=1
+                )
+                low_all[h, at_row, :] = low.astype(bf16)
+
+        prompt_load(step + SLOTS).start()
+    for k in range(1, heads):
+        send(low_all.at[h], low_all.at[h], "zl", k - 1, {"head": (h + k) % heads})
+
+    def base_loop(ch, first, ready):
+        @pl.loop(0, requests)
+        def _(r):
+            step = first + r
+            prompt_load(step).wait()
+
+            @pl.loop(0, tiles)
+            def _(i):
+                at_row = pl.ds(pl.multiple_of(i * TILE, TILE), TILE)
+                weight = w[ch][pl.ds(pl.multiple_of(y * half_width, half_width), half_width), :]
+                acc[r, at_row, :] = jnp.dot(
+                    pbuf[step % SLOTS, at_row, :], weight, preferred_element_type=f32
+                )
+
+            prompt_load(step + SLOTS).start()
+
+    order_row = lax.broadcasted_iota(jnp.int32, (2 * PART, 2 * PART), 0)
+    order_col = lax.broadcasted_iota(jnp.int32, (2 * PART, 2 * PART), 1)
+    order = jnp.where(order_col == (order_row % 2) * PART + order_row // 2, 1.0, 0.0).astype(bf16)
+
+    def final_loop(ch, first):
+        lanes = slice(ch * PART, (ch + 1) * PART)
+
+        @pl.loop(0, requests)
+        def _(r):
+            step = first + r
+            prompt_load(step).wait()
+            adapter = adapter_ref[r]
+            up_key, up_value = up_ref[adapter, 0][:, lanes], up_ref[adapter, 1][:, lanes]
+            gap = jnp.zeros_like(up_key)
+            up = jnp.concatenate(
+                [
+                    jnp.concatenate([up_key, gap], axis=1),
+                    jnp.concatenate([gap, up_value], axis=1),
+                    jnp.zeros((PART - columns, 2 * PART), bf16),
+                ],
+                axis=0,
+            )
+
+            @pl.loop(0, tiles)
+            def _(i):
+                at_row = pl.ds(pl.multiple_of(i * TILE, TILE), TILE)
+                weight = w[ch][
+                    pl.ds(pl.multiple_of((1 - y) * half_width, half_width), half_width), :
+                ]
+                value = (
+                    acc[r, at_row, :]
+                    + jnp.dot(
+                        pbuf[step % SLOTS, at_row, :], weight, preferred_element_type=f32
+                    )
+                    + jnp.dot(low_all[r, at_row, :], up, preferred_element_type=f32)
+                ).astype(bf16)
+                for sub in range(TILE // PART):
+                    x = value[sub * PART : (sub + 1) * PART]
+                    both = jnp.concatenate([x[:, :PART], x[:, PART:]], axis=0)
+                    woven = jnp.dot(order, both, preferred_element_type=f32).astype(bf16)
+                    hsend[
+                        ch, r,
+                        pl.ds(pl.multiple_of(2 * (i * TILE + sub * PART), 2 * PART), 2 * PART), :,
+                    ] = woven
+
+            remote(
+                hsend.at[ch, r], recvx[ch].at[r], "hx", ch * requests + r, to_x
+            ).start()
+
+            @pl.when(step + SLOTS < total_steps)
+            def _():
+                prompt_load(step + SLOTS).start()
+
+    own_a.wait()
+    arrive(rows_of(w0, sib * shard, shard), "sa", 0, to_sib)
+    base_loop(0, 2, None)
+    for k in range(PIECES):
+        x_arrived(k)
+    peer_other = rows_of(w0, peer * shard + (1 - p) * half_shard, half_shard)
+    send(peer_other, peer_other, "fa", 1, to_sib)
+    for k in range(1, heads):
+        source = (h + heads - k) % heads
+        arrive(low_all.at[source], "zl", k - 1, {"head": source})
+    for k in range(2):
+        pool_part = p + k - 2 * k * p
+        arrive(rows_of(w0, far * shard + pool_part * half_shard, half_shard), "fa", k, to_sib)
+    final_loop(0, 2 + requests)
+
+    arrive(att_all.at[peer], "yt", 0, to_peer)
+    send(att_all.at[peer], att_all.at[peer], "ft", 0, to_sib)
+    arrive(att_all.at[sib], "st", 0, to_sib)
+    arrive(att_all.at[far], "ft", 0, to_sib)
+    members = att_all.shape[0]
+    attended = att_all[...].reshape(members * rows, q_heads * HEAD_DIM)
+    low_rows = lax.dot_general(
+        attended, odown_ref[...], (((1,), (1,)), ((), ())), preferred_element_type=f32
+    )
+    low_rows = jnp.where(keep_ref[...] > 0.5, low_rows, 0.0).astype(bf16)
+    ow_width = owbuf.shape[2]
+    blocks = ow_ref.shape[1] // ow_width
+
+    @pl.loop(0, blocks)
+    def _(n):
+        ow_load(n).wait()
+        cols = pl.ds(pl.multiple_of(n * ow_width, ow_width), ow_width)
+        part = jnp.dot(
+            att_all[...].reshape(members * rows, q_heads * HEAD_DIM), owbuf[n % 2],
+            preferred_element_type=f32,
+        ) + jnp.dot(low_rows, oup_ref[:, cols], preferred_element_type=f32)
+        terms[:, :, cols] = part.reshape(heads, rows, ow_width)
+
+        @pl.when(n + 2 < blocks)
+        def _():
+            ow_load(n + 2).start()
+
+    for k in range(1, heads):
+        target = (h + k) % heads
+        tsend[k - 1] = terms[target].astype(bf16)
+        send(tsend.at[k - 1], trecv.at[k - 1], "zt", k - 1, {"head": target})
+
+    arrive(rows_of(w1, sib * shard, shard), "sb", 0, to_sib)
+    own_b.wait()
+    base_loop(1, 2 + 2 * requests, None)
+
+    base = (1 - p) * requests
+    owner = [dest_ref[base + r] for r in range(requests)]
+    away = [jnp.where(owner[r] // 2 == y, 0, 1) for r in range(requests)]
+
+    def passed_home(j):
+        kept = 1 - away[0]
+        for r in range(1, j + 1):
+            kept = jnp.maximum(kept, 1 - away[r])
+        return kept
+
+    def passed_away(j):
+        kept = away[0]
+        for r in range(1, j + 1):
+            kept = jnp.maximum(kept, away[r])
+        return kept
+
+    chosen = []
+    for s in range(CAP):
+        index, found = 0, 0
+        for r in range(requests):
+            before = sum([jnp.where(owner[q] == owner[r], 1, 0) for q in range(r)], 0)
+            hit = jnp.where((owner[r] == me) & (before == s), 1, 0)
+            shift = passed_away(r - 1) if r > 0 else 0
+            index = index + hit * r
+            found = found + hit
+            chosen_slot = hit * (r - shift)
+            if r == 0:
+                slot = chosen_slot
+            else:
+                slot = slot + chosen_slot
+        chosen.append((found, index, jnp.clip(slot, 0, slots - 1)))
+
+    def on_x(ch, r):
+        arrive(recvx[ch].at[r], "hx", ch * requests + r, to_x)
+        send(recvx[ch].at[r], sibx[ch].at[r], "hs", ch * requests + r, to_sib)
+        if r >= 1:
+            j = r - 1
+            late = jnp.full((1, 1), passed_home(j), jnp.int32) > 0
+            ysend[ch * slots + j] = jnp.where(late, recvx[ch][r], recvx[ch][j])
+            send(ysend.at[ch * slots + j], yrecv[ch].at[j], "hy", ch * slots + j, to_peer)
+
+    def on_y(ch, j):
+        arrive(yrecv[ch].at[j], "hy", ch * slots + j, to_peer)
+        send(yrecv[ch].at[j], siby[ch].at[j], "hf", ch * slots + j, to_sib)
+
+    def place(ch, source, ref, by_slot):
+        for s, (found, index, slot) in enumerate(chosen):
+            got = jnp.full((1, 1), found, jnp.int32) > 0
+            value = ref[slot if by_slot else index]
+            out_ref[s, source, ch] = jnp.where(got, value, jnp.zeros_like(value))
+
+    def place_x(ch):
+        for r in range(requests):
+            arrive(sibx[ch].at[r], "hs", ch * requests + r, to_sib)
+        place(ch, me, recvx[ch], False)
+        place(ch, sib, sibx[ch], False)
+
+    def place_y(ch):
+        for j in range(slots):
+            arrive(siby[ch].at[j], "hf", ch * slots + j, to_sib)
+        place(ch, peer, yrecv[ch], True)
+        place(ch, far, siby[ch], True)
+
+    def wb_arrived(k):
+        part = rows_of(w1, peer * shard + k * half_shard, half_shard)
+        arrive(part, "yb", k, to_peer)
+        send(part, part, "fb", k, to_sib)
+
+    on_x(0, 0)
+    wb_arrived(0)
+    total = terms[h]
+    for k in range(1, heads):
+        arrive(trecv.at[k - 1], "zt", k - 1, {"head": (h + heads - k) % heads})
+        total = total + trecv[k - 1].astype(f32)
+    decoded_ref[...] = total.astype(bf16)
+    for r in range(1, requests):
+        on_x(0, r)
+    wb_arrived(1)
+    for k in range(2):
+        arrive(rows_of(w1, far * shard + k * half_shard, half_shard), "fb", k, to_sib)
+    final_loop(1, 2 + 3 * requests)
+    on_y(0, 0)
+    on_x(1, 0)
+    on_y(0, 1)
+    on_x(1, 1)
+    for j in range(2, slots):
+        on_y(0, j)
+    place_x(0)
+    place_y(0)
+    for r in range(2, requests):
+        on_x(1, r)
+        on_y(1, r - 2)
+    place_x(1)
+    on_y(1, slots - 1)
+    place_y(1)
+
+    for ch in range(2):
+        for r in range(requests):
+            remote(
+                hsend.at[ch, r], recvx[ch].at[r], "hx", ch * requests + r, to_x
+            ).wait_send()
+    for copy in sent:
+        copy.wait_send()
+
+
+def serve(
+    prompt, key_value_weight, adapter_down_weight, adapter_up_weight, request_adapter_index,
+    destination, rotated_query, key_value_cache, current_key_value, cached_length,
+    row_adapter_index, output_weight, output_down_weight, output_up_weight,
+):
+    f32, bf16 = jnp.float32, jnp.bfloat16
+    requests, tok, model = prompt.shape
+    shard, _, width = key_value_weight.shape
+    heads = lax.axis_size("head")
+    members = lax.axis_size("seq")
+    rows = rotated_query.shape[0]
+    attn_width = rotated_query.shape[1]
+    q_heads = attn_width // HEAD_DIM
+    ranks = ADAPTER_COUNT * ADAPTER_RANK
+    out_width = output_weight.shape[1]
+    wa = key_value_weight[:, :, :PART].reshape(shard, 2 * PART)
+    wb = key_value_weight[:, :, PART:].reshape(shard, 2 * PART)
+    odown = output_down_weight.transpose(1, 2, 0).reshape(ranks, attn_width)
+    oup = output_up_weight.reshape(ranks, out_width)
+    rank_owner = jnp.arange(ranks, dtype=jnp.int32) // ADAPTER_RANK
+    keep = (row_adapter_index[:, None] == rank_owner[None, :]).astype(f32)
+    slots = requests - 1
+    ow_width = out_width // 4
+    block = (2 * tok, PART)
+    sems = 64 + 8 * requests
+    vmem, smem, hbm = (
+        pl.BlockSpec(memory_space=pltpu.VMEM),
+        pl.BlockSpec(memory_space=pltpu.SMEM),
+        pl.BlockSpec(memory_space=pl.ANY),
+    )
+    out, decoded = pl.pallas_call(
+        serve_kernel,
+        in_specs=[smem, smem, smem, hbm, hbm, hbm, vmem, vmem, vmem, hbm, vmem, vmem, hbm, vmem, vmem],
+        out_specs=[vmem, vmem],
+        out_shape=[
+            jax.ShapeDtypeStruct((CAP, members, 2) + block, bf16),
+            jax.ShapeDtypeStruct((rows, out_width), bf16),
+        ],
+        scratch_shapes=[
+            pltpu.VMEM((model, 2 * PART), bf16),
+            pltpu.VMEM((model, 2 * PART), bf16),
+            pltpu.VMEM((SLOTS, tok, 2 * shard), bf16),
+            pltpu.VMEM((requests, tok, 2 * PART), f32),
+            pltpu.VMEM(key_value_cache.shape, bf16),
+            pltpu.VMEM((2, attn_width, ow_width), bf16),
+            pltpu.VMEM((rows * q_heads, HEAD_DIM), f32),
+            pltpu.VMEM((rows * q_heads, HEAD_DIM), f32),
+            pltpu.VMEM((members, rows, attn_width), bf16),
+            pltpu.VMEM((2 * ADAPTER_RANK, model), bf16),
+            pltpu.VMEM((tok, 2 * ADAPTER_RANK), f32),
+            pltpu.VMEM((requests, tok, PART), bf16),
+            pltpu.VMEM((heads, rows, out_width), f32),
+            pltpu.VMEM((heads - 1, rows, out_width), bf16),
+            pltpu.VMEM((heads - 1, rows, out_width), bf16),
+            pltpu.VMEM((2, requests) + block, bf16),
+            pltpu.VMEM((requests,) + block, bf16),
+            pltpu.VMEM((requests,) + block, bf16),
+            pltpu.VMEM((requests,) + block, bf16),
+            pltpu.VMEM((requests,) + block, bf16),
+            pltpu.VMEM((2 * slots,) + block, bf16),
+            pltpu.VMEM((slots,) + block, bf16),
+            pltpu.VMEM((slots,) + block, bf16),
+            pltpu.VMEM((slots,) + block, bf16),
+            pltpu.VMEM((slots,) + block, bf16),
+            pltpu.SemaphoreType.DMA((sems,)),
+            pltpu.SemaphoreType.DMA((sems,)),
+            pltpu.SemaphoreType.DMA((SLOTS + 5,)),
+        ],
+        compiler_params=pltpu.CompilerParams(
+            collective_id=0, has_side_effects=True, vmem_limit_bytes=67043328
+        ),
+    )(
+        destination, request_adapter_index, cached_length, prompt, wa, wb, adapter_down_weight,
+        adapter_up_weight, rotated_query, key_value_cache, current_key_value, keep, output_weight,
+        odown, oup,
+    )
+    handed = out.reshape(CAP, members, 2, tok, 2, PART).transpose(0, 1, 3, 4, 2, 5)
+    return handed.reshape(1, CAP, members * tok, 2, width), decoded
+
+
+def fits(mesh):
+    return mesh.shape["seq"] == 4 and mesh.shape["pool"] == 2
+
+
 def solution(mesh):
     in_specs = (
         P("pool", "seq", None),
@@ -291,4 +890,5 @@
         P(None, None, "seq"),
     )
     out_specs = (P(("pool", "seq"), None, None, None, "head"), P(("pool", "head"), "seq"))
-    return jax.shard_map(body, mesh=mesh, in_specs=in_specs, out_specs=out_specs, check_vma=False)
+    run = serve if fits(mesh) else body
+    return jax.shard_map(run, mesh=mesh, in_specs=in_specs, out_specs=out_specs, check_vma=False)

time: 194 us -> 142 us (0.73)
  the two profiles are of different devices: /device:TPU:1 before, /device:TPU:29 now
where the time goes in v1:
time: 142 us
  Pallas kernels  112 us (79%)
  local copies, waits for them, and re-layouts  27.5 us (19%)
  other arithmetic  1.42 us (1%)
    pallas_call x1, Pallas kernels, serve(): pl.pallas_call(serve_kernel, in_specs=[smem, smem, smem, hbm, hbm, hbm, v...  112 us
    reshape x1, local copies, waits for them, and re-layouts, serve(): return (handed.reshape(1, CAP, members * tok, 2, width), decoded)  11.7 us
    transpose x1, local copies, waits for them, and re-layouts, serve(): out.reshape(CAP, members, 2, tok, 2, PART).transpose(0, 1, 3, 4, 2, 5)  10.6 us

profile of v1, /device:TPU:29, one launch (start us, length us, event | category | flops | bytes accessed | tf_op | source)
XLA Modules:
  0.0 141.8 jit_solution(7162542056595224269)
XLA Ops:
  0.6 1.4 compare_convert_fusion.keep_ref
  2.1 2.7 %fusion = (bf16[2048,2,128]{2,1,0:T(2,128)(2,1)S(1)}, bf16[2048,2,128]{2,1,0:T(2,128)(2,1)S(1)}) fusion(bf16[2048,2,256]{2,1,0:T(2,128)(2,1)} %param.15), kind=kLoop, calls=%fused_computation.7 | loop fusion | bytes 4194304 | tf_op jit(solution)/shard_map/slice | solution.py:807
  4.7 1.7 %copy_bitcast_fusion = (bf16[2048,256]{1,0:T(8,128)(2,1)}, bf16[2048,256]{1,0:T(8,128)(2,1)}) fusion(bf16[256,8,2,128]{3,2,1,0:T(2,128)(2,1)S(1)} %bitcast.14, bf16[256,8,2,128]{3,2,1,0:T(2,128)(2,1)S(1)} %bitcast.15), kind=kLoop, calls=%fused_computation | loop fusion | bytes 4194304 | tf_op jit(solution)/shard_map/reshape | solution.py:807
  6.5 112.2 %shard_map.149 = (bf16[2,4,2,1024,128]{4,3,2,1,0:T(8,128)(2,1)}, bf16[48,2048]{1,0:T(8,128)(2,1)}) custom-call(s32[8]{0:T(128)} %dest_ref.1, s32[4]{0:T(128)} %adapter_ref.1, s32[48]{0:T(128)} %length_ref.1, bf16[4,512,8192]{2,1,0:T(8,128)(2,1)} %prompt_ref.1, bf16[2048,256]{1,0:T(8,128)(2,1)} %get-tuple-element.9.wa_ref, ...), custom_call_target="tpu_custom_call" | custom-call | tf_op jit(solution)/shard_map/pallas_call | solution.py:821
  118.7 10.6 %copy.16 = bf16[2,4,512,2,2,128]{5,4,3,2,1,0:T(2,128)(2,1)} copy(bf16[2,4,512,2,2,128]{5,3,2,4,1,0:T(2,128)(2,1)} %bitcast.13) | data formatting | bytes 8388608 | tf_op jit(solution)/shard_map/transpose | solution.py:867
  129.4 0.0 copy-start
  129.4 11.7 %reshape.41 = bf16[1,2,2048,2,256]{4,3,2,1,0:T(2,128)(2,1)} reshape(bf16[2,4,512,2,2,128]{5,4,3,2,1,0:T(2,128)(2,1)} %copy.16) | data formatting | bytes 8388608 | tf_op jit(solution)/shard_map/reshape | solution.py:868
  141.1 0.0 copy-done
  141.1 0.7 copy.22
  (1 shorter events, 0.0 us)
Async XLA Ops:
  129.4 11.7 %copy-start = (bf16[48,2048]{1,0:T(8,128)(2,1)S(1)}, bf16[48,2048]{1,0:T(8,128)(2,1)}, u32[]{:S(2)}) copy-start(bf16[48,2048]{1,0:T(8,128)(2,1)} %get-tuple-element.13) | copy-start | bytes 589828

commit v2 on v0

--- a/solution.py
+++ b/solution.py
@@ -273,6 +273,768 @@
     return (weave(handed[0], handed[1]), decoded)
 
 
+MESH = pl.DeviceIdType.MESH
+PIECES = 4
+SLOTS = 3
+SHARED = 1
+OUTS = 8
+TILE = 256
+PART = 128
+
+
+def serve_kernel(
+    dest_ref,
+    adapter_ref,
+    length_ref,
+    prompt_ref,
+    kv_ref,
+    down_hbm,
+    up_hbm,
+    query_hbm,
+    cache_ref,
+    current_hbm,
+    row_ref,
+    ow_ref,
+    odown_hbm,
+    oup_hbm,
+    out_ref,
+    decoded_ref,
+    w0,
+    w1,
+    kraw,
+    pbuf,
+    acc,
+    cbuf,
+    owbuf,
+    down_ref,
+    up_ref,
+    query_ref,
+    current_ref,
+    odown_ref,
+    oup_ref,
+    qbuf,
+    abuf,
+    att_all,
+    down_all,
+    low_acc,
+    low_flat,
+    low_all,
+    terms,
+    tsend,
+    trecv,
+    hsend,
+    stage,
+    recvx0,
+    recvx1,
+    sibx0,
+    sibx1,
+    ysend,
+    yrecv0,
+    yrecv1,
+    siby0,
+    siby1,
+    ssem,
+    rsem,
+    lsem,
+):
+    f32, bf16 = jnp.float32, jnp.bfloat16
+    requests, tok, model = prompt_ref.shape
+    shard = kv_ref.shape[0]
+    half_width = 2 * shard
+    heads = lax.axis_size("head")
+    rows = query_ref.shape[0]
+    q_heads = query_ref.shape[1] // HEAD_DIM
+    columns = 2 * ADAPTER_RANK
+    p, me, h = lax.axis_index("pool"), lax.axis_index("seq"), lax.axis_index("head")
+    y, c = me // 2, me % 2
+    sib, peer, far = y * 2 + 1 - c, (1 - y) * 2 + c, (1 - y) * 2 + 1 - c
+    slots = requests - 1
+    tiles = tok // TILE
+    recvx, sibx = (recvx0, recvx1), (sibx0, sibx1)
+    yrecv, siby = (yrecv0, yrecv1), (siby0, siby1)
+    w = (w0, w1)
+
+    names, at = {}, 0
+    for name, count in (
+        ("ya", PIECES), ("xa", PIECES), ("sa", 1), ("fa", 2 * PIECES),
+        ("yb", SHARED + 1), ("xb", SHARED), ("sb", 1), ("fb", 3),
+        ("yd", 1), ("sd", 1), ("fd", 1), ("yt", 1), ("st", 1), ("ft", 1),
+        ("zl", heads - 1), ("zt", heads - 1),
+        ("hx", 2 * requests * tiles), ("hs", 2 * requests * tiles),
+        ("hy", 2 * slots * tiles), ("hf", 2 * slots * tiles),
+    ):
+        names[name] = at
+        at += count
+
+    sent = []
+
+    def remote(src, dst, name, index, target):
+        i = names[name] + index
+        return pltpu.make_async_remote_copy(
+            src_ref=src, dst_ref=dst, send_sem=ssem.at[i], recv_sem=rsem.at[i],
+            device_id=target, device_id_type=MESH,
+        )
+
+    def send(src, dst, name, index, target):
+        copy = remote(src, dst, name, index, target)
+        copy.start()
+        sent.append(copy)
+
+    def arrive(dst, name, index, target):
+        remote(dst, dst, name, index, target).wait_recv()
+
+    to_sib, to_peer, to_x = {"seq": sib}, {"seq": peer}, {"pool": 1 - p}
+
+    def rows_of(ref, start, size):
+        return ref.at[pl.ds(pl.multiple_of(start, PART), size)]
+
+    def pass_on(part, name, index, target):
+        send(part, part, name, index, target)
+
+    def kv_load(ch):
+        return pltpu.make_async_copy(
+            kv_ref.at[:, :, ch * PART : (ch + 1) * PART], kraw.at[ch], lsem.at[SLOTS + 1 + ch]
+        )
+
+    ends = SLOTS + 5 + OUTS
+    small = [
+        pltpu.make_async_copy(src, dst, lsem.at[ends + i])
+        for i, (src, dst) in enumerate(
+            (
+                (down_hbm, down_ref), (up_hbm, up_ref), (query_hbm, query_ref),
+                (current_hbm, current_ref), (odown_hbm, odown_ref), (oup_hbm, oup_ref),
+            )
+        )
+    ]
+
+    def prompt_load(step):
+        if isinstance(step, int) and step < requests:
+            r, half = step, y
+        elif isinstance(step, int) and step < requests + 2:
+            r, half = h, (y if step == requests else 1 - y)
+        else:
+            t = step - 2
+            r, turn = t % requests, (t // requests) % 2
+            half = turn + y - 2 * turn * y
+        slot = step % SLOTS
+        return pltpu.make_async_copy(
+            prompt_ref.at[r, :, pl.ds(pl.multiple_of(half * half_width, half_width), half_width)],
+            pbuf.at[slot],
+            lsem.at[slot],
+        )
+
+    def ow_load(n):
+        width = owbuf.shape[2]
+        return pltpu.make_async_copy(
+            ow_ref.at[:, pl.ds(pl.multiple_of(n * width, width), width)],
+            owbuf.at[n % 2],
+            lsem.at[SLOTS + 3 + n % 2],
+        )
+
+    total_steps = 2 + 4 * requests
+    kv_load(0).start()
+    small[0].start()
+
+    barrier = pltpu.get_barrier_semaphore()
+    partners = [to_sib, to_peer, to_x] + [{"head": (h + k) % heads} for k in range(1, heads)]
+    for partner in partners:
+        pl.semaphore_signal(barrier, inc=1, device_id=partner, device_id_type=MESH)
+    prompt_load(0).start()
+    kv_load(1).start()
+    for step in range(1, SLOTS):
+        prompt_load(step).start()
+    for copy in small[1:]:
+        copy.start()
+    cache_copy = pltpu.make_async_copy(cache_ref, cbuf, lsem.at[SLOTS])
+    cache_copy.start()
+    ow_load(0).start()
+    ow_load(1).start()
+
+    order_row = lax.broadcasted_iota(jnp.int32, (2 * PART, 2 * PART), 0)
+    order_col = lax.broadcasted_iota(jnp.int32, (2 * PART, 2 * PART), 1)
+    order = jnp.where(order_col == (order_row % 2) * PART + order_row // 2, 1.0, 0.0).astype(bf16)
+    unorder = jnp.where(order_row == (order_col % 2) * PART + order_col // 2, 1.0, 0.0).astype(bf16)
+
+    def split_rows(ch, start, size):
+        @pl.loop(0, size // PART)
+        def _(b):
+            row = pl.multiple_of(start + b * PART, PART)
+            pairs = kraw[ch, pl.ds(row, PART)].reshape(2 * PART, PART)
+            parts = jnp.dot(unorder, pairs, preferred_element_type=f32).astype(bf16)
+            to = pl.ds(pl.multiple_of(me * shard + row, PART), PART)
+            w[ch][to, :PART] = parts[:PART]
+            w[ch][to, PART:] = parts[PART:]
+
+    piece = shard // (2 * PIECES)
+    half_shard = shard // 2
+
+    def y_piece(k):
+        pass_on(rows_of(w0, me * shard + (p * PIECES + k) * piece, piece), "ya", k, to_peer)
+
+    def y_arrived(k):
+        part = rows_of(w0, peer * shard + (p * PIECES + k) * piece, piece)
+        arrive(part, "ya", k, to_peer)
+        pass_on(part, "xa", k, to_x)
+        pass_on(part, "fa", k, to_sib)
+
+    def x_arrived(k):
+        part = rows_of(w0, peer * shard + ((1 - p) * PIECES + k) * piece, piece)
+        arrive(part, "xa", k, to_x)
+        pass_on(part, "fa", PIECES + k, to_sib)
+
+    def far_arrived():
+        for k in range(PIECES):
+            for turn, pool_part in enumerate((p, 1 - p)):
+                part = rows_of(w0, far * shard + (pool_part * PIECES + k) * piece, piece)
+                arrive(part, "fa", turn * PIECES + k, to_sib)
+
+    kv_load(0).wait()
+    split_rows(0, p * half_shard, 2 * piece)
+    pl.semaphore_wait(barrier, len(partners))
+    y_piece(0)
+    split_rows(0, p * half_shard + 2 * piece, 2 * piece)
+    y_piece(1)
+
+    small[0].wait()
+    pick_row = lax.broadcasted_iota(jnp.int32, (columns, down_ref.shape[1]), 0)
+    pick_col = lax.broadcasted_iota(jnp.int32, (columns, down_ref.shape[1]), 1)
+    pick = jnp.where(pick_col == pick_row + adapter_ref[h] * columns, 1.0, 0.0).astype(bf16)
+
+    def cols_at(who):
+        return down_all.at[:, pl.ds(pl.multiple_of(who * shard, shard), shard)]
+
+    down_all[:, pl.ds(pl.multiple_of(me * shard, shard), shard)] = lax.dot_general(
+        pick, down_ref[...], (((1,), (1,)), ((), ())), preferred_element_type=f32
+    ).astype(bf16)
+    split_rows(0, (1 - p) * half_shard, half_shard)
+    pass_on(cols_at(me), "yd", 0, to_peer)
+    pass_on(cols_at(me), "sd", 0, to_sib)
+    y_piece(2)
+    y_piece(3)
+    pass_on(rows_of(w0, me * shard, shard), "sa", 0, to_sib)
+
+    def base(ch, r, step):
+        prompt_load(step).wait()
+
+        @pl.loop(0, tiles)
+        def _(i):
+            at_row = pl.ds(pl.multiple_of(i * TILE, TILE), TILE)
+            weight = w[ch][pl.ds(pl.multiple_of(y * half_width, half_width), half_width), :]
+            acc[r, at_row, :] = jnp.dot(
+                pbuf[step % SLOTS, at_row, :], weight, preferred_element_type=f32
+            )
+
+        prompt_load(step + SLOTS).start()
+
+    kv_load(1).wait()
+    kept = shard - 2 * SHARED * piece
+    mine_at = p * (shard - SHARED * piece)
+    theirs_at = (1 - p) * (shard - SHARED * piece)
+    split_rows(1, mine_at, SHARED * piece)
+    for k in range(SHARED):
+        pass_on(rows_of(w1, me * shard + mine_at + k * piece, piece), "yb", k, to_peer)
+    split_rows(1, SHARED * piece, kept)
+    pass_on(rows_of(w1, me * shard + SHARED * piece, kept), "yb", SHARED, to_peer)
+    split_rows(1, theirs_at, SHARED * piece)
+
+    arrive(rows_of(w0, sib * shard, shard), "sa", 0, to_sib)
+    base(0, 0, 0)
+    y_arrived(0)
+    base(0, 1, 1)
+    y_arrived(1)
+    base(0, 2, 2)
+    arrive(cols_at(peer), "yd", 0, to_peer)
+    pass_on(cols_at(peer), "fd", 0, to_sib)
+    for r in range(3, requests):
+        base(0, r, r)
+    y_arrived(2)
+
+    pass_on(rows_of(w1, me * shard, shard), "sb", 0, to_sib)
+    arrive(cols_at(sib), "sd", 0, to_sib)
+    arrive(cols_at(far), "fd", 0, to_sib)
+
+    for turn in range(2):
+        step = requests + turn
+        prompt_load(step).wait()
+        half = y if turn == 0 else 1 - y
+        cols = pl.ds(pl.multiple_of(half * half_width, half_width), half_width)
+
+        @pl.loop(0, tiles)
+        def _(i):
+            at_row = pl.ds(pl.multiple_of(i * TILE, TILE), TILE)
+            part = lax.dot_general(
+                pbuf[step % SLOTS, at_row, :], down_all[:, cols], (((1,), (1,)), ((), ())),
+                preferred_element_type=f32,
+            )
+            if turn == 0:
+                low_acc[at_row, :] = part
+            else:
+                low = jnp.concatenate(
+                    [low_acc[at_row, :] + part, jnp.zeros((TILE, PART - columns), f32)], axis=1
+                )
+                low_flat[h, i] = low.T[:columns].astype(bf16)
+
+        prompt_load(step + SLOTS).start()
+    for k in range(1, heads):
+        pass_on(low_flat.at[h], "zl", k - 1, {"head": (h + k) % heads})
+    y_arrived(3)
+    for copy in small[1:]:
+        copy.wait()
+
+    def half_block(ref, index, i):
+        return ref.at[index, pl.ds(pl.multiple_of(i * 2 * TILE, 2 * TILE), 2 * TILE)]
+
+    def final(ch, r, step):
+        lanes = slice(ch * PART, (ch + 1) * PART)
+        prompt_load(step).wait()
+        adapter = adapter_ref[r]
+        up_key, up_value = up_ref[adapter, 0][:, lanes], up_ref[adapter, 1][:, lanes]
+        gap = jnp.zeros_like(up_key)
+        up = jnp.concatenate(
+            [
+                jnp.concatenate([up_key, gap], axis=1),
+                jnp.concatenate([gap, up_value], axis=1),
+                jnp.zeros((PART - columns, 2 * PART), bf16),
+            ],
+            axis=0,
+        )
+
+        @pl.loop(0, tiles)
+        def _(i):
+            at_row = pl.ds(pl.multiple_of(i * TILE, TILE), TILE)
+            weight = w[ch][
+                pl.ds(pl.multiple_of((1 - y) * half_width, half_width), half_width), :
+            ]
+            value = (
+                acc[r, at_row, :]
+                + jnp.dot(pbuf[step % SLOTS, at_row, :], weight, preferred_element_type=f32)
+                + jnp.dot(low_all[r, at_row, :], up, preferred_element_type=f32)
+            ).astype(bf16)
+            for sub in range(TILE // PART):
+                x = value[sub * PART : (sub + 1) * PART]
+                both = jnp.concatenate([x[:, :PART], x[:, PART:]], axis=0)
+                woven = jnp.dot(order, both, preferred_element_type=f32).astype(bf16)
+                hsend[
+                    ch * requests + r,
+                    pl.ds(pl.multiple_of(2 * (i * TILE + sub * PART), 2 * PART), 2 * PART), :,
+                ] = woven
+            remote(
+                half_block(hsend, ch * requests + r, i), half_block(recvx[ch], r, i),
+                "hx", (ch * requests + r) * tiles + i, to_x,
+            ).start()
+
+        if step + SLOTS < total_steps:
+            prompt_load(step + SLOTS).start()
+
+    for head in range(q_heads):
+        qbuf[pl.ds(head, rows, stride=q_heads), :] = query_ref[
+            :, head * HEAD_DIM : (head + 1) * HEAD_DIM
+        ].astype(f32)
+    cache_copy.wait()
+    positions = cache_ref.shape[1]
+    kv_heads = current_ref.shape[2] // HEAD_DIM
+    groups = q_heads // kv_heads
+    batch = 8
+    factor = HEAD_DIM ** (-0.5)
+    lane = lax.broadcasted_iota(jnp.int32, (groups, 2 * positions), 1)
+
+    batches = rows // batch
+
+    def attend_step(step):
+        start = step * batch
+        blocks, scores, owns, values = [], [], [], []
+        for row in range(batch):
+            pairs = cbuf[start + row].reshape(2 * positions, kv_heads * HEAD_DIM)
+            valid = (lane % 2 == 0) & (lane < 2 * length_ref[start + row])
+            now = current_ref[start + row].astype(f32)
+            for head in range(kv_heads):
+                span = slice(head * HEAD_DIM, (head + 1) * HEAD_DIM)
+                block = pairs[:, span]
+                query = qbuf[
+                    pl.ds(pl.multiple_of((start + row) * q_heads + head * groups, groups), groups), :
+                ]
+                own = jnp.sum(query * now[0:1, span], axis=1, keepdims=True) * factor
+                score = lax.dot_general(
+                    query.astype(bf16), block, (((1,), (1,)), ((), ())), preferred_element_type=f32
+                )
+                blocks.append(block)
+                scores.append(jnp.where(valid, score * factor, -1e30))
+                owns.append(own)
+                values.append(now[1:2, span])
+        score = jnp.concatenate(scores, axis=0)
+        own = jnp.concatenate(owns, axis=0)
+        highest = jnp.maximum(jnp.max(score, axis=1, keepdims=True), own)
+        raw = jnp.where(score > -1e29, jnp.exp(score - highest), 0.0)
+        own_raw = jnp.exp(own - highest)
+        normer = jnp.sum(raw, axis=1, keepdims=True) + own_raw
+        weights = pltpu.roll(raw / normer, 1, 1).astype(bf16)
+        own_weight = (own_raw / normer).astype(bf16).astype(f32)
+        for item in range(batch * kv_heads):
+            at_row = item * groups
+            mixed = jnp.dot(
+                weights[at_row : at_row + groups], blocks[item], preferred_element_type=f32
+            )
+            abuf[
+                pl.ds(pl.multiple_of(start * q_heads + at_row, groups), groups), :
+            ] = mixed + own_weight[at_row : at_row + groups] * values[item]
+
+    def attend(start, stop):
+        pl.loop(start, stop)(attend_step)
+
+    attend(0, batches // 3)
+    for k in range(PIECES - 1):
+        x_arrived(k)
+    attend(batches // 3, batches - batches // 3)
+    x_arrived(PIECES - 1)
+    for k in range(1, heads):
+        source = (h + heads - k) % heads
+        arrive(low_flat.at[source], "zl", k - 1, {"head": source})
+
+    @pl.loop(0, requests)
+    def _(r):
+        for i in range(tiles):
+            low = jnp.concatenate(
+                [low_flat[r, i].astype(f32), jnp.zeros((PART - columns, TILE), f32)], axis=0
+            )
+            low_all[r, i * TILE : (i + 1) * TILE, :] = low.T.astype(bf16)
+
+    far_arrived()
+
+    def shared_arrived(k):
+        part = rows_of(w1, peer * shard + mine_at + k * piece, piece)
+        arrive(part, "yb", k, to_peer)
+        pass_on(part, "xb", k, to_x)
+
+    first = 2 + requests
+    for r in range(requests):
+        final(0, r, first + r)
+        if r < SHARED:
+            shared_arrived(r)
+    pass_on(rows_of(w1, peer * shard + mine_at, SHARED * piece), "fb", 0, to_sib)
+
+    attend(batches - batches // 3, batches)
+    for head in range(q_heads):
+        att_all[me, :, head * HEAD_DIM : (head + 1) * HEAD_DIM] = abuf[
+            pl.ds(head, rows, stride=q_heads), :
+        ].astype(bf16)
+    pass_on(att_all.at[me], "yt", 0, to_peer)
+    pass_on(att_all.at[me], "st", 0, to_sib)
+
+    other = (1 - p) * requests
+    owner = [dest_ref[other + r] for r in range(requests)]
+    away = [jnp.where(owner[r] // 2 == y, 0, 1) for r in range(requests)]
+
+    def some(flags):
+        kept = flags[0]
+        for flag in flags[1:]:
+            kept = jnp.maximum(kept, flag)
+        return kept
+
+    chosen = []
+    for s in range(CAP):
+        index, found, slot = 0, 0, 0
+        for r in range(requests):
+            before = sum([jnp.where(owner[q] == owner[r], 1, 0) for q in range(r)], 0)
+            hit = jnp.where((owner[r] == me) & (before == s), 1, 0)
+            shift = some(away[:r]) if r > 0 else 0
+            index, found, slot = index + hit * r, found + hit, slot + hit * (r - shift)
+        chosen.append((found, index, jnp.clip(slot, 0, slots - 1)))
+
+    def on_x(ch, r, i):
+        part = half_block(recvx[ch], r, i)
+        arrive(part, "hx", (ch * requests + r) * tiles + i, to_x)
+        send(part, half_block(sibx[ch], r, i), "hs", (ch * requests + r) * tiles + i, to_sib)
+        if r >= 1:
+            j = r - 1
+            span = slice(i * 2 * TILE, (i + 1) * 2 * TILE)
+            late = jnp.full((1, 1), some([1 - a for a in away[: j + 1]]), jnp.int32) > 0
+            ysend[ch * slots + j, span] = jnp.where(late, recvx[ch][r, span], recvx[ch][j, span])
+            send(
+                half_block(ysend, ch * slots + j, i), half_block(yrecv[ch], j, i),
+                "hy", (ch * slots + j) * tiles + i, to_peer,
+            )
+
+    def on_y(ch, j, i):
+        part = half_block(yrecv[ch], j, i)
+        arrive(part, "hy", (ch * slots + j) * tiles + i, to_peer)
+        send(part, half_block(siby[ch], j, i), "hf", (ch * slots + j) * tiles + i, to_sib)
+
+    placed = []
+
+    def place(ch, source, ref, by_slot, i):
+        span = pl.ds(i * 2 * TILE, 2 * TILE)
+        for s, (found, index, slot) in enumerate(chosen):
+            got = jnp.full((1, 1), found, jnp.int32) > 0
+            value = ref[slot if by_slot else index, span]
+            turn = len(placed)
+            if turn >= OUTS:
+                placed[turn - OUTS].wait()
+            stage[turn % OUTS] = jnp.where(got, value, jnp.zeros_like(value))
+            copy = pltpu.make_async_copy(
+                stage.at[turn % OUTS], out_ref.at[s, source, ch, span],
+                lsem.at[SLOTS + 5 + turn % OUTS],
+            )
+            copy.start()
+            placed.append(copy)
+
+    def place_x(ch):
+        for i in range(tiles):
+            place(ch, me, recvx[ch], False, i)
+        for r in range(requests):
+            for i in range(tiles):
+                arrive(half_block(sibx[ch], r, i), "hs", (ch * requests + r) * tiles + i, to_sib)
+        for i in range(tiles):
+            place(ch, sib, sibx[ch], False, i)
+
+    def place_y(ch):
+        for i in range(tiles):
+            place(ch, peer, yrecv[ch], True, i)
+        for j in range(slots):
+            for i in range(tiles):
+                arrive(half_block(siby[ch], j, i), "hf", (ch * slots + j) * tiles + i, to_sib)
+        for i in range(tiles):
+            place(ch, far, siby[ch], True, i)
+
+    x_queue = [(ch, r, i) for ch in range(2) for r in range(requests) for i in range(tiles)]
+    y_queue = [(ch, j, i) for ch in range(2) for j in range(slots) for i in range(tiles)]
+
+    def take_x(count):
+        for _ in range(count):
+            on_x(*x_queue.pop(0))
+
+    def take_y(count):
+        for _ in range(count):
+            on_y(*y_queue.pop(0))
+
+    def project():
+        arrive(att_all.at[sib], "st", 0, to_sib)
+        arrive(att_all.at[far], "ft", 0, to_sib)
+        members = att_all.shape[0]
+        low_rows = lax.dot_general(
+            odown_ref[...], att_all[...].reshape(members * rows, q_heads * HEAD_DIM),
+            (((1,), (1,)), ((), ())), preferred_element_type=f32,
+        )
+        rank_owner = lax.broadcasted_iota(jnp.int32, low_rows.shape, 0) // ADAPTER_RANK
+        low_rows = jnp.where(rank_owner == row_ref[...], low_rows, 0.0).astype(bf16)
+        ow_width = owbuf.shape[2]
+        blocks = ow_ref.shape[1] // ow_width
+
+        @pl.loop(0, blocks)
+        def _(n):
+            ow_load(n).wait()
+            cols = pl.ds(pl.multiple_of(n * ow_width, ow_width), ow_width)
+            part = jnp.dot(
+                att_all[...].reshape(members * rows, q_heads * HEAD_DIM), owbuf[n % 2],
+                preferred_element_type=f32,
+            ) + lax.dot_general(
+                low_rows, oup_ref[:, cols], (((0,), (0,)), ((), ())), preferred_element_type=f32
+            )
+            terms[:, :, cols] = part.reshape(heads, rows, ow_width)
+
+            @pl.when(n + 2 < blocks)
+            def _():
+                ow_load(n + 2).start()
+
+        for k in range(1, heads):
+            target = (h + k) % heads
+            tsend[k - 1] = terms[target].astype(bf16)
+            send(tsend.at[k - 1], trecv.at[k - 1], "zt", k - 1, {"head": target})
+
+    take_x(tiles)
+    arrive(rows_of(w1, sib * shard, shard), "sb", 0, to_sib)
+    first = 2 + 2 * requests
+    for r in range(requests):
+        base(1, r, first + r)
+    part = rows_of(w1, peer * shard + SHARED * piece, kept)
+    arrive(part, "yb", SHARED, to_peer)
+    pass_on(part, "fb", 1, to_sib)
+    for k in range(SHARED):
+        arrive(rows_of(w1, peer * shard + theirs_at + k * piece, piece), "xb", k, to_x)
+    pass_on(rows_of(w1, peer * shard + theirs_at, SHARED * piece), "fb", 2, to_sib)
+    take_x(tiles)
+    arrive(rows_of(w1, far * shard + mine_at, SHARED * piece), "fb", 0, to_sib)
+    arrive(rows_of(w1, far * shard + SHARED * piece, kept), "fb", 1, to_sib)
+    arrive(rows_of(w1, far * shard + theirs_at, SHARED * piece), "fb", 2, to_sib)
+    first = 2 + 3 * requests
+    final(1, 0, first)
+    final(1, 1, first + 1)
+    take_x(1)
+    arrive(att_all.at[peer], "yt", 0, to_peer)
+    pass_on(att_all.at[peer], "ft", 0, to_sib)
+    for r in range(2, requests - 1):
+        final(1, r, first + r)
+    take_x(1)
+    project()
+    take_x(1)
+    final(1, requests - 1, first + requests - 1)
+    while x_queue[0][0] == 0:
+        take_x(1)
+    take_y(2 * tiles)
+    take_x(tiles)
+    while y_queue[0][0] == 0:
+        take_y(1)
+    take_x(tiles)
+    place_x(0)
+    place_y(0)
+    while len(x_queue) > tiles:
+        take_x(1)
+        take_y(1)
+    take_x(1)
+    take_y(1)
+    total = terms[h]
+    for k in range(1, heads):
+        arrive(trecv.at[k - 1], "zt", k - 1, {"head": (h + heads - k) % heads})
+        total = total + trecv[k - 1].astype(f32)
+    decoded_ref[...] = total.astype(bf16)
+    while x_queue:
+        take_x(1)
+    place_x(1)
+    while y_queue:
+        take_y(1)
+    place_y(1)
+
+    for ch in range(2):
+        for r in range(requests):
+            for i in range(tiles):
+                remote(
+                    half_block(hsend, ch * requests + r, i), half_block(recvx[ch], r, i),
+                    "hx", (ch * requests + r) * tiles + i, to_x,
+                ).wait_send()
+    for copy in sent:
+        copy.wait_send()
+    for copy in placed[-OUTS:]:
+        copy.wait()
+
+
+def serve(
+    prompt, key_value_weight, adapter_down_weight, adapter_up_weight, request_adapter_index,
+    destination, rotated_query, key_value_cache, current_key_value, cached_length,
+    row_adapter_index, output_weight, output_down_weight, output_up_weight,
+):
+    f32, bf16 = jnp.float32, jnp.bfloat16
+    requests, tok, model = prompt.shape
+    shard, _, width = key_value_weight.shape
+    heads = lax.axis_size("head")
+    members = lax.axis_size("seq")
+    rows = rotated_query.shape[0]
+    attn_width = rotated_query.shape[1]
+    q_heads = attn_width // HEAD_DIM
+    ranks = ADAPTER_COUNT * ADAPTER_RANK
+    out_width = output_weight.shape[1]
+    odown = output_down_weight.transpose(1, 2, 0).reshape(ranks, attn_width)
+    oup = output_up_weight.reshape(ranks, out_width)
+    slots = requests - 1
+    ow_width = out_width // 4
+    block = (2 * tok, PART)
+    tiles = tok // TILE
+    sems = 64 + 8 * requests * tiles
+    vmem, smem, hbm = (
+        pl.BlockSpec(memory_space=pltpu.VMEM),
+        pl.BlockSpec(memory_space=pltpu.SMEM),
+        pl.BlockSpec(memory_space=pl.ANY),
+    )
+    out, decoded = pl.pallas_call(
+        serve_kernel,
+        in_specs=[smem, smem, smem, hbm, hbm, hbm, hbm, hbm, hbm, hbm, vmem, hbm, hbm, hbm],
+        out_specs=[hbm, vmem],
+        out_shape=[
+            jax.ShapeDtypeStruct((CAP, members, 2) + block, bf16),
+            jax.ShapeDtypeStruct((rows, out_width), bf16),
+        ],
+        scratch_shapes=[
+            pltpu.VMEM((model, 2 * PART), bf16),
+            pltpu.VMEM((model, 2 * PART), bf16),
+            pltpu.VMEM((2, shard, 2, PART), bf16),
+            pltpu.VMEM((SLOTS, tok, 2 * shard), bf16),
+            pltpu.VMEM((requests, tok, 2 * PART), f32),
+            pltpu.VMEM(key_value_cache.shape, bf16),
+            pltpu.VMEM((2, attn_width, ow_width), bf16),
+            pltpu.VMEM(adapter_down_weight.shape, bf16),
+            pltpu.VMEM(adapter_up_weight.shape, bf16),
+            pltpu.VMEM(rotated_query.shape, bf16),
+            pltpu.VMEM(current_key_value.shape, bf16),
+            pltpu.VMEM(odown.shape, bf16),
+            pltpu.VMEM(oup.shape, bf16),
+            pltpu.VMEM((rows * q_heads, HEAD_DIM), f32),
+            pltpu.VMEM((rows * q_heads, HEAD_DIM), f32),
+            pltpu.VMEM((members, rows, attn_width), bf16),
+            pltpu.VMEM((2 * ADAPTER_RANK, model), bf16),
+            pltpu.VMEM((tok, 2 * ADAPTER_RANK), f32),
+            pltpu.VMEM((requests, tiles, 2 * ADAPTER_RANK, TILE), bf16),
+            pltpu.VMEM((requests, tok, PART), bf16),
+            pltpu.VMEM((heads, rows, out_width), f32),
+            pltpu.VMEM((heads - 1, rows, out_width), bf16),
+            pltpu.VMEM((heads - 1, rows, out_width), bf16),
+            pltpu.VMEM((2 * requests,) + block, bf16),
+            pltpu.VMEM((OUTS, 2 * TILE, PART), bf16),
+            pltpu.VMEM((requests,) + block, bf16),
+            pltpu.VMEM((requests,) + block, bf16),
+            pltpu.VMEM((requests,) + block, bf16),
+            pltpu.VMEM((requests,) + block, bf16),
+            pltpu.VMEM((2 * slots,) + block, bf16),
+            pltpu.VMEM((slots,) + block, bf16),
+            pltpu.VMEM((slots,) + block, bf16),
+            pltpu.VMEM((slots,) + block, bf16),
+            pltpu.VMEM((slots,) + block, bf16),
+            pltpu.SemaphoreType.DMA((sems,)),
+            pltpu.SemaphoreType.DMA((sems,)),
+            pltpu.SemaphoreType.DMA((SLOTS + 11 + OUTS,)),
+        ],
+        compiler_params=pltpu.CompilerParams(
+            collective_id=0, has_side_effects=True, vmem_limit_bytes=67043328
+        ),
+    )(
+        destination, request_adapter_index, cached_length, prompt, key_value_weight, adapter_down_weight,
+        adapter_up_weight, rotated_query, key_value_cache, current_key_value,
+        row_adapter_index.reshape(1, -1), output_weight,
+        odown, oup,
+    )
+    return join(out.reshape(CAP, members, 2, tok, 2, PART)), decoded
+
+
+def join_kernel(in_ref, out_ref, buf, in_sem, out_sem):
+    slots, members, halves, tok, _, lanes = in_ref.shape
+    places = [(s, m, k) for s in range(slots) for m in range(members) for k in range(halves)]
+    loads = [
+        pltpu.make_async_copy(in_ref.at[place], buf.at[i], in_sem.at[i])
+        for i, place in enumerate(places)
+    ]
+    for copy in loads:
+        copy.start()
+    stores = []
+    for i, (s, m, k) in enumerate(places):
+        loads[i].wait()
+        copy = pltpu.make_async_copy(
+            buf.at[i],
+            out_ref.at[0, s, pl.ds(m * tok, tok), :, pl.ds(k * lanes, lanes)],
+            out_sem.at[i],
+        )
+        copy.start()
+        stores.append(copy)
+    for copy in stores:
+        copy.wait()
+
+
+def join(blocks):
+    slots, members, halves, tok, pair, lanes = blocks.shape
+    count = slots * members * halves
+    return pl.pallas_call(
+        join_kernel,
+        in_specs=[pl.BlockSpec(memory_space=pl.ANY)],
+        out_specs=pl.BlockSpec(memory_space=pl.ANY),
+        out_shape=jax.ShapeDtypeStruct((1, slots, members * tok, pair, halves * lanes), blocks.dtype),
+        scratch_shapes=[
+            pltpu.VMEM((count, tok, pair, lanes), blocks.dtype),
+            pltpu.SemaphoreType.DMA((count,)),
+            pltpu.SemaphoreType.DMA((count,)),
+        ],
+    )(blocks)
+
+
+def fits(mesh):
+    return mesh.shape["seq"] == 4 and mesh.shape["pool"] == 2
+
+
 def solution(mesh):
     in_specs = (
         P("pool", "seq", None),
@@ -291,4 +1053,5 @@
         P(None, None, "seq"),
     )
     out_specs = (P(("pool", "seq"), None, None, None, "head"), P(("pool", "head"), "seq"))
-    return jax.shard_map(body, mesh=mesh, in_specs=in_specs, out_specs=out_specs, check_vma=False)
+    run = serve if fits(mesh) else body
+    return jax.shard_map(run, mesh=mesh, in_specs=in_specs, out_specs=out_specs, check_vma=False)

time: 194 us -> 94.3 us (0.49)
  Pallas kernels: 16.9 us -> 92.7 us
  waiting for transfers between devices: 62.3 us -> 0 us
  matrix products: 48.2 us -> 0 us
  starting transfers between devices: 29.2 us -> 0 us
  other arithmetic: 17.7 us -> 0 us
  local copies, waits for them, and re-layouts: 16.5 us -> 0.68 us
    pallas_call x2, Pallas kernels: 16.9 us -> 92.7 us  [the longest x1 88.9 us: serve(): pl.pallas_call(serve_kernel, in_specs=[smem, smem, smem, hbm, hbm, hbm, h...]
    ppermute x14 -> x0, waiting for transfers between devices: 53.1 us -> none  [exchanged(): return lax.ppermute(value, axis, pairs)]
    dot_general x9 -> x0, matrix products: 48.2 us -> none  [the longest x2 32.4 us: body(): base = jnp.dot(tokens, weight, preferred_element_type=jnp.float32)]
    ppermute x14 -> x0, starting transfers between devices: 18 us -> none  [exchanged(): return lax.ppermute(value, axis, pairs)]
    all_to_all x2 -> x0, starting transfers between devices: 11.2 us -> none  [hand_over(): lax.all_to_all(outgoing, 'seq', split_axis=0, concat_axis=0, tiled=True)]
    all_to_all x2 -> x0, waiting for transfers between devices: 9.21 us -> none  [hand_over(): lax.all_to_all(outgoing, 'seq', split_axis=0, concat_axis=0, tiled=True)]
    another operation x15 -> x0, other arithmetic: 8.12 us -> none  [gathered(): held = jnp.stack([first, second], axis=1).reshape((-1,) + value.shape)]
    select_n x6 -> x0, other arithmetic: 4.65 us -> none  [the longest x2 3.74 us: hand_over(): jnp.where(hits[:, :, request][:, :, None, None], arrived[request][None, N...]
  transfers between devices with their start and end apart: 16 -> 0, of which waited for: 9 -> 0; matrix products, arithmetic and copies ran while one was open for 40% -> 0% of each run, Pallas kernels for 5% -> 0%
where the time goes in v2:
time: 94.3 us; the launch traced here: 94.1 us
  Pallas kernels  92.7 us (98%)
    pallas_call x1, Pallas kernels, serve(): pl.pallas_call(serve_kernel, in_specs=[smem, smem, smem, hbm, hbm, hbm, h...  88.9 us
    pallas_call x1, Pallas kernels, join(): pl.pallas_call(join_kernel, in_specs=[pl.BlockSpec(memory_space=pl.ANY)],...  3.89 us

profile of v2, /device:TPU:1, one launch (start us, length us, event | category | flops | bytes accessed | tf_op | source)
XLA Modules:
  0.0 94.1 jit_solution(4589358736492315540)
XLA Ops:
  0.6 88.9 %shard_map.149 = (bf16[2,4,2,1024,128]{4,3,2,1,0:T(8,128)(2,1)}, bf16[48,2048]{1,0:T(8,128)(2,1)}) custom-call(s32[8]{0:T(128)} %dest_ref.1, s32[4]{0:T(128)} %adapter_ref.1, s32[48]{0:T(128)} %length_ref.1, bf16[4,512,8192]{2,1,0:T(8,128)(2,1)} %prompt_ref.1, bf16[2048,2,256]{2,1,0:T(2,128)(2,1)} %kv_ref.1, bf16[2048,256]{1,0:T(8,128)(2,1)} %down_hbm.1, ...), custom_call_target="tpu_custom_call" | custom-call | tf_op jit(solution)/shard_map/pallas_call | solution.py:936
  89.5 0.0 copy-start
  89.5 3.9 %shard_map.150 = bf16[1,2,2048,2,256]{4,3,2,1,0:T(2,128)(2,1)} custom-call(bf16[2,4,2,512,2,128]{5,4,3,2,1,0:T(2,128)(2,1)} %bitcast.6), custom_call_target="tpu_custom_call" | custom-call | tf_op jit(solution)/shard_map/pallas_call | solution.py:1021
  93.4 0.0 copy-done
  93.4 0.7 copy.17
Async XLA Ops:
  89.5 3.9 %copy-start = (bf16[48,2048]{1,0:T(8,128)(2,1)S(1)}, bf16[48,2048]{1,0:T(8,128)(2,1)}, u32[]{:S(2)}) copy-start(bf16[48,2048]{1,0:T(8,128)(2,1)} %get-tuple-element.9) | copy-start | bytes 589828

commit v3 on v2

--- a/solution.py
+++ b/solution.py
@@ -274,7 +274,7 @@
 
 
 MESH = pl.DeviceIdType.MESH
-PIECES = 4
+PIECES = 8
 SLOTS = 3
 SHARED = 1
 OUTS = 8
@@ -322,6 +322,7 @@
     terms,
     tsend,
     trecv,
+    decoded,
     hsend,
     stage,
     recvx0,
@@ -360,8 +361,8 @@
         ("yb", SHARED + 1), ("xb", SHARED), ("sb", 1), ("fb", 3),
         ("yd", 1), ("sd", 1), ("fd", 1), ("yt", 1), ("st", 1), ("ft", 1),
         ("zl", heads - 1), ("zt", heads - 1),
-        ("hx", 2 * requests * tiles), ("hs", 2 * requests * tiles),
-        ("hy", 2 * slots * tiles), ("hf", 2 * slots * tiles),
+        ("hx", 2 * requests * tiles + 1), ("hs", 2 * requests * tiles + 1),
+        ("hy", 2 * slots * tiles + 1), ("hf", 2 * slots * tiles + 1),
     ):
         names[name] = at
         at += count
@@ -489,11 +490,10 @@
                 arrive(part, "fa", turn * PIECES + k, to_sib)
 
     kv_load(0).wait()
-    split_rows(0, p * half_shard, 2 * piece)
+    split_rows(0, p * half_shard, half_shard)
     pl.semaphore_wait(barrier, len(partners))
-    y_piece(0)
-    split_rows(0, p * half_shard + 2 * piece, 2 * piece)
-    y_piece(1)
+    for k in range(PIECES // 2):
+        y_piece(k)
 
     small[0].wait()
     pick_row = lax.broadcasted_iota(jnp.int32, (columns, down_ref.shape[1]), 0)
@@ -509,8 +509,8 @@
     split_rows(0, (1 - p) * half_shard, half_shard)
     pass_on(cols_at(me), "yd", 0, to_peer)
     pass_on(cols_at(me), "sd", 0, to_sib)
-    y_piece(2)
-    y_piece(3)
+    for k in range(PIECES // 2, PIECES):
+        y_piece(k)
     pass_on(rows_of(w0, me * shard, shard), "sa", 0, to_sib)
 
     def base(ch, r, step):
@@ -530,30 +530,34 @@
     kept = shard - 2 * SHARED * piece
     mine_at = p * (shard - SHARED * piece)
     theirs_at = (1 - p) * (shard - SHARED * piece)
-    split_rows(1, mine_at, SHARED * piece)
+    if SHARED:
+        split_rows(1, mine_at, SHARED * piece)
     for k in range(SHARED):
         pass_on(rows_of(w1, me * shard + mine_at + k * piece, piece), "yb", k, to_peer)
     split_rows(1, SHARED * piece, kept)
     pass_on(rows_of(w1, me * shard + SHARED * piece, kept), "yb", SHARED, to_peer)
-    split_rows(1, theirs_at, SHARED * piece)
+    if SHARED:
+        split_rows(1, theirs_at, SHARED * piece)
 
     arrive(rows_of(w0, sib * shard, shard), "sa", 0, to_sib)
+    for k in range(PIECES // 2 - 1):
+        y_arrived(k)
     base(0, 0, 0)
-    y_arrived(0)
+    y_arrived(PIECES // 2 - 1)
     base(0, 1, 1)
-    y_arrived(1)
     base(0, 2, 2)
     arrive(cols_at(peer), "yd", 0, to_peer)
     pass_on(cols_at(peer), "fd", 0, to_sib)
     for r in range(3, requests):
         base(0, r, r)
-    y_arrived(2)
+    y_arrived(PIECES // 2)
 
     pass_on(rows_of(w1, me * shard, shard), "sb", 0, to_sib)
     arrive(cols_at(sib), "sd", 0, to_sib)
     arrive(cols_at(far), "fd", 0, to_sib)
 
     for turn in range(2):
+        y_arrived(PIECES // 2 + 1 + turn)
         step = requests + turn
         prompt_load(step).wait()
         half = y if turn == 0 else 1 - y
@@ -577,12 +581,23 @@
         prompt_load(step + SLOTS).start()
     for k in range(1, heads):
         pass_on(low_flat.at[h], "zl", k - 1, {"head": (h + k) % heads})
-    y_arrived(3)
+    for k in range(PIECES // 2 + 3, PIECES):
+        y_arrived(k)
     for copy in small[1:]:
         copy.wait()
 
-    def half_block(ref, index, i):
-        return ref.at[index, pl.ds(pl.multiple_of(i * 2 * TILE, 2 * TILE), 2 * TILE)]
+    def spans(ch, r):
+        if ch == 1 and r == requests - 1:
+            ends_at = [0] + [(i + 1) * TILE for i in range(tiles - 1)] + [tok - PART, tok]
+        else:
+            ends_at = [i * TILE for i in range(tiles + 1)]
+        return [(2 * a, 2 * (b - a)) for a, b in zip(ends_at, ends_at[1:])]
+
+    def part_of(ref, index, span):
+        return ref.at[index, pl.ds(span[0], span[1])]
+
+    def sem_at(ch, r, i):
+        return (ch * requests + r) * tiles + i
 
     def final(ch, r, step):
         lanes = slice(ch * PART, (ch + 1) * PART)
@@ -618,11 +633,19 @@
                     ch * requests + r,
                     pl.ds(pl.multiple_of(2 * (i * TILE + sub * PART), 2 * PART), 2 * PART), :,
                 ] = woven
-            remote(
-                half_block(hsend, ch * requests + r, i), half_block(recvx[ch], r, i),
-                "hx", (ch * requests + r) * tiles + i, to_x,
-            ).start()
-
+            if (ch, r) != (1, requests - 1):
+                span = (pl.multiple_of(i * 2 * TILE, 2 * TILE), 2 * TILE)
+                remote(
+                    part_of(hsend, ch * requests + r, span), part_of(recvx[ch], r, span),
+                    "hx", sem_at(ch, r, i), to_x,
+                ).start()
+
+        if (ch, r) == (1, requests - 1):
+            for i, span in enumerate(spans(ch, r)):
+                remote(
+                    part_of(hsend, ch * requests + r, span), part_of(recvx[ch], r, span),
+                    "hx", sem_at(ch, r, i), to_x,
+                ).start()
         if step + SLOTS < total_steps:
             prompt_load(step + SLOTS).start()
 
@@ -681,11 +704,13 @@
     def attend(start, stop):
         pl.loop(start, stop)(attend_step)
 
+    for k in range(PIECES // 2):
+        x_arrived(k)
     attend(0, batches // 3)
-    for k in range(PIECES - 1):
+    for k in range(PIECES // 2, PIECES - 1):
         x_arrived(k)
-    attend(batches // 3, batches - batches // 3)
     x_arrived(PIECES - 1)
+    attend(batches // 3, batches // 2)
     for k in range(1, heads):
         source = (h + heads - k) % heads
         arrive(low_flat.at[source], "zl", k - 1, {"head": source})
@@ -710,9 +735,10 @@
         final(0, r, first + r)
         if r < SHARED:
             shared_arrived(r)
-    pass_on(rows_of(w1, peer * shard + mine_at, SHARED * piece), "fb", 0, to_sib)
-
-    attend(batches - batches // 3, batches)
+    if SHARED:
+        pass_on(rows_of(w1, peer * shard + mine_at, SHARED * piece), "fb", 0, to_sib)
+
+    attend(batches // 2, batches)
     for head in range(q_heads):
         att_all[me, :, head * HEAD_DIM : (head + 1) * HEAD_DIM] = abuf[
             pl.ds(head, rows, stride=q_heads), :
@@ -741,23 +767,26 @@
         chosen.append((found, index, jnp.clip(slot, 0, slots - 1)))
 
     def on_x(ch, r, i):
-        part = half_block(recvx[ch], r, i)
-        arrive(part, "hx", (ch * requests + r) * tiles + i, to_x)
-        send(part, half_block(sibx[ch], r, i), "hs", (ch * requests + r) * tiles + i, to_sib)
+        span = spans(ch, r)[i]
+        part = part_of(recvx[ch], r, span)
+        arrive(part, "hx", sem_at(ch, r, i), to_x)
+        send(part, part_of(sibx[ch], r, span), "hs", sem_at(ch, r, i), to_sib)
         if r >= 1:
-            j = r - 1
-            span = slice(i * 2 * TILE, (i + 1) * 2 * TILE)
+            j, k = r - 1, sem_at(ch, r - 1, i) - ch * tiles
+            at_row = slice(span[0], span[0] + span[1])
             late = jnp.full((1, 1), some([1 - a for a in away[: j + 1]]), jnp.int32) > 0
-            ysend[ch * slots + j, span] = jnp.where(late, recvx[ch][r, span], recvx[ch][j, span])
+            ysend[ch * slots + j, at_row] = jnp.where(
+                late, recvx[ch][r, at_row], recvx[ch][j, at_row]
+            )
             send(
-                half_block(ysend, ch * slots + j, i), half_block(yrecv[ch], j, i),
-                "hy", (ch * slots + j) * tiles + i, to_peer,
+                part_of(ysend, ch * slots + j, span), part_of(yrecv[ch], j, span), "hy", k, to_peer
             )
 
     def on_y(ch, j, i):
-        part = half_block(yrecv[ch], j, i)
-        arrive(part, "hy", (ch * slots + j) * tiles + i, to_peer)
-        send(part, half_block(siby[ch], j, i), "hf", (ch * slots + j) * tiles + i, to_sib)
+        span = spans(ch, j + 1)[i]
+        part, k = part_of(yrecv[ch], j, span), sem_at(ch, j, i) - ch * tiles
+        arrive(part, "hy", k, to_peer)
+        send(part, part_of(siby[ch], j, span), "hf", k, to_sib)
 
     placed = []
 
@@ -781,8 +810,8 @@
         for i in range(tiles):
             place(ch, me, recvx[ch], False, i)
         for r in range(requests):
-            for i in range(tiles):
-                arrive(half_block(sibx[ch], r, i), "hs", (ch * requests + r) * tiles + i, to_sib)
+            for i, span in enumerate(spans(ch, r)):
+                arrive(part_of(sibx[ch], r, span), "hs", sem_at(ch, r, i), to_sib)
         for i in range(tiles):
             place(ch, sib, sibx[ch], False, i)
 
@@ -790,13 +819,17 @@
         for i in range(tiles):
             place(ch, peer, yrecv[ch], True, i)
         for j in range(slots):
-            for i in range(tiles):
-                arrive(half_block(siby[ch], j, i), "hf", (ch * slots + j) * tiles + i, to_sib)
+            for i, span in enumerate(spans(ch, j + 1)):
+                arrive(part_of(siby[ch], j, span), "hf", sem_at(ch, j, i) - ch * tiles, to_sib)
         for i in range(tiles):
             place(ch, far, siby[ch], True, i)
 
-    x_queue = [(ch, r, i) for ch in range(2) for r in range(requests) for i in range(tiles)]
-    y_queue = [(ch, j, i) for ch in range(2) for j in range(slots) for i in range(tiles)]
+    x_queue = [
+        (ch, r, i) for ch in range(2) for r in range(requests) for i in range(len(spans(ch, r)))
+    ]
+    y_queue = [
+        (ch, j, i) for ch in range(2) for j in range(slots) for i in range(len(spans(ch, j + 1)))
+    ]
 
     def take_x(count):
         for _ in range(count):
@@ -819,8 +852,7 @@
         ow_width = owbuf.shape[2]
         blocks = ow_ref.shape[1] // ow_width
 
-        @pl.loop(0, blocks)
-        def _(n):
+        def step(n):
             ow_load(n).wait()
             cols = pl.ds(pl.multiple_of(n * ow_width, ow_width), ow_width)
             part = jnp.dot(
@@ -835,59 +867,72 @@
             def _():
                 ow_load(n + 2).start()
 
+        pl.loop(0, blocks // 2)(step)
+        take_x(1)
+        pl.loop(blocks // 2, blocks)(step)
+
         for k in range(1, heads):
             target = (h + k) % heads
             tsend[k - 1] = terms[target].astype(bf16)
             send(tsend.at[k - 1], trecv.at[k - 1], "zt", k - 1, {"head": target})
 
     take_x(tiles)
+    for k in range(SHARED):
+        arrive(rows_of(w1, peer * shard + theirs_at + k * piece, piece), "xb", k, to_x)
+    if SHARED:
+        pass_on(rows_of(w1, peer * shard + theirs_at, SHARED * piece), "fb", 2, to_sib)
     arrive(rows_of(w1, sib * shard, shard), "sb", 0, to_sib)
     first = 2 + 2 * requests
     for r in range(requests):
         base(1, r, first + r)
-    part = rows_of(w1, peer * shard + SHARED * piece, kept)
-    arrive(part, "yb", SHARED, to_peer)
-    pass_on(part, "fb", 1, to_sib)
-    for k in range(SHARED):
-        arrive(rows_of(w1, peer * shard + theirs_at + k * piece, piece), "xb", k, to_x)
-    pass_on(rows_of(w1, peer * shard + theirs_at, SHARED * piece), "fb", 2, to_sib)
-    take_x(tiles)
-    arrive(rows_of(w1, far * shard + mine_at, SHARED * piece), "fb", 0, to_sib)
+        if r == requests - 2:
+            part = rows_of(w1, peer * shard + SHARED * piece, kept)
+            arrive(part, "yb", SHARED, to_peer)
+            pass_on(part, "fb", 1, to_sib)
+            take_x(1)
+    take_x(tiles - 1)
+    if SHARED:
+        arrive(rows_of(w1, far * shard + mine_at, SHARED * piece), "fb", 0, to_sib)
+        arrive(rows_of(w1, far * shard + theirs_at, SHARED * piece), "fb", 2, to_sib)
     arrive(rows_of(w1, far * shard + SHARED * piece, kept), "fb", 1, to_sib)
-    arrive(rows_of(w1, far * shard + theirs_at, SHARED * piece), "fb", 2, to_sib)
     first = 2 + 3 * requests
     final(1, 0, first)
+    take_x(1)
     final(1, 1, first + 1)
     take_x(1)
     arrive(att_all.at[peer], "yt", 0, to_peer)
     pass_on(att_all.at[peer], "ft", 0, to_sib)
     for r in range(2, requests - 1):
         final(1, r, first + r)
-    take_x(1)
+        take_x(1)
     project()
-    take_x(1)
     final(1, requests - 1, first + requests - 1)
     while x_queue[0][0] == 0:
         take_x(1)
-    take_y(2 * tiles)
+
     take_x(tiles)
+    for i in range(tiles):
+        while len([item for item in y_queue if item[0] == 0]) > tiles - i:
+            take_y(1)
+        take_x(1)
     while y_queue[0][0] == 0:
         take_y(1)
-    take_x(tiles)
     place_x(0)
     place_y(0)
-    while len(x_queue) > tiles:
-        take_x(1)
-        take_y(1)
+    for r in range(2, requests - 1):
+        take_x(tiles)
+        take_y(tiles)
     take_x(1)
     take_y(1)
+    while x_queue:
+        take_x(1)
     total = terms[h]
     for k in range(1, heads):
         arrive(trecv.at[k - 1], "zt", k - 1, {"head": (h + heads - k) % heads})
         total = total + trecv[k - 1].astype(f32)
-    decoded_ref[...] = total.astype(bf16)
-    while x_queue:
-        take_x(1)
+    decoded[...] = total.astype(bf16)
+    decoded_copy = pltpu.make_async_copy(decoded, decoded_ref, lsem.at[ends + len(small)])
+    decoded_copy.start()
     place_x(1)
     while y_queue:
         take_y(1)
@@ -895,15 +940,16 @@
 
     for ch in range(2):
         for r in range(requests):
-            for i in range(tiles):
+            for i, span in enumerate(spans(ch, r)):
                 remote(
-                    half_block(hsend, ch * requests + r, i), half_block(recvx[ch], r, i),
-                    "hx", (ch * requests + r) * tiles + i, to_x,
+                    part_of(hsend, ch * requests + r, span), part_of(recvx[ch], r, span),
+                    "hx", sem_at(ch, r, i), to_x,
                 ).wait_send()
     for copy in sent:
         copy.wait_send()
     for copy in placed[-OUTS:]:
         copy.wait()
+    decoded_copy.wait()
 
 
 def serve(
@@ -927,7 +973,7 @@
     ow_width = out_width // 4
     block = (2 * tok, PART)
     tiles = tok // TILE
-    sems = 64 + 8 * requests * tiles
+    sems = 96 + 8 * requests * tiles
     vmem, smem, hbm = (
         pl.BlockSpec(memory_space=pltpu.VMEM),
         pl.BlockSpec(memory_space=pltpu.SMEM),
@@ -936,7 +982,7 @@
     out, decoded = pl.pallas_call(
         serve_kernel,
         in_specs=[smem, smem, smem, hbm, hbm, hbm, hbm, hbm, hbm, hbm, vmem, hbm, hbm, hbm],
-        out_specs=[hbm, vmem],
+        out_specs=[hbm, hbm],
         out_shape=[
             jax.ShapeDtypeStruct((CAP, members, 2) + block, bf16),
             jax.ShapeDtypeStruct((rows, out_width), bf16),
@@ -965,6 +1011,7 @@
             pltpu.VMEM((heads, rows, out_width), f32),
             pltpu.VMEM((heads - 1, rows, out_width), bf16),
             pltpu.VMEM((heads - 1, rows, out_width), bf16),
+            pltpu.VMEM((rows, out_width), bf16),
             pltpu.VMEM((2 * requests,) + block, bf16),
             pltpu.VMEM((OUTS, 2 * TILE, PART), bf16),
             pltpu.VMEM((requests,) + block, bf16),
@@ -978,7 +1025,7 @@
             pltpu.VMEM((slots,) + block, bf16),
             pltpu.SemaphoreType.DMA((sems,)),
             pltpu.SemaphoreType.DMA((sems,)),
-            pltpu.SemaphoreType.DMA((SLOTS + 11 + OUTS,)),
+            pltpu.SemaphoreType.DMA((SLOTS + 12 + OUTS,)),
         ],
         compiler_params=pltpu.CompilerParams(
             collective_id=0, has_side_effects=True, vmem_limit_bytes=67043328

time: 94.3 us -> 92 us (0.976)
  Pallas kernels: 92.7 us -> 90.5 us
    pallas_call x1, Pallas kernels: 88.9 us -> 86.6 us  [serve(): pl.pallas_call(serve_kernel, in_specs=[smem, smem, smem, hbm, hbm, hbm, h...]
where the time goes in v3:
time: 92 us; the launch traced here: 91.9 us
  Pallas kernels  90.5 us (98%)
    pallas_call x1, Pallas kernels, serve(): pl.pallas_call(serve_kernel, in_specs=[smem, smem, smem, hbm, hbm, hbm, h...  86.6 us
    pallas_call x1, Pallas kernels, join(): pl.pallas_call(join_kernel, in_specs=[pl.BlockSpec(memory_space=pl.ANY)],...  3.89 us

profile of v3, /device:TPU:1, one launch (start us, length us, event | category | flops | bytes accessed | tf_op | source)
XLA Modules:
  0.0 91.9 jit_solution(3494060648056189484)
XLA Ops:
  0.6 86.6 %shard_map.149 = (bf16[2,4,2,1024,128]{4,3,2,1,0:T(8,128)(2,1)}, bf16[48,2048]{1,0:T(8,128)(2,1)}) custom-call(s32[8]{0:T(128)} %dest_ref.1, s32[4]{0:T(128)} %adapter_ref.1, s32[48]{0:T(128)} %length_ref.1, bf16[4,512,8192]{2,1,0:T(8,128)(2,1)} %prompt_ref.1, bf16[2048,2,256]{2,1,0:T(2,128)(2,1)} %kv_ref.1, bf16[2048,256]{1,0:T(8,128)(2,1)} %down_hbm.1, ...), custom_call_target="tpu_custom_call" | custom-call | tf_op jit(solution)/shard_map/pallas_call | solution.py:982
  87.3 0.0 copy-start
  87.3 3.9 %shard_map.150 = bf16[1,2,2048,2,256]{4,3,2,1,0:T(2,128)(2,1)} custom-call(bf16[2,4,2,512,2,128]{5,4,3,2,1,0:T(2,128)(2,1)} %bitcast.6), custom_call_target="tpu_custom_call" | custom-call | tf_op jit(solution)/shard_map/pallas_call | solution.py:1068
  91.2 0.0 copy-done
  91.2 0.7 copy.17
Async XLA Ops:
  87.3 3.9 %copy-start = (bf16[48,2048]{1,0:T(8,128)(2,1)S(1)}, bf16[48,2048]{1,0:T(8,128)(2,1)}, u32[]{:S(2)}) copy-start(bf16[48,2048]{1,0:T(8,128)(2,1)} %get-tuple-element.9) | copy-start | bytes 589828
